TPU v7x, 32 devices: a whole 2x2x4 slice. The times are simulated.
32 devices in a mesh: ga: 8 (over y, x, core), band: 4 (over z).
Axes of the slice: x: 2, y: 2, z: 4, core: 2. Of those that a mesh axis runs over, the one named last changes fastest.
Arguments:
- psi: bfloat16 [2, 8, 96, 2048], P(None, 'band', None, 'ga'), may hold values from -6 to 6
- vloc: float32 [96, 9216], P('ga'), may hold values from 0.5 to 1.5
- dv: float32 [96, 9216], P('ga'), may hold values from -6 to 6
- beta: float32 [2, 128, 96, 2048], P(None, None, None, 'ga'), may hold values from -0.02734375 to 0.02734375
- dij: float32 [2, 4, 4], replicated, may hold values from -1 to 1.5, as said below
- atom_type: int32 [32], replicated, may hold values from 0 to 1
- stick_xy: int32 [2048], replicated, may hold values from 0 to 9215, as said below
- band_shift: float32 [8], P('band'), may hold values from 0.3 to 3
Outputs:
- response: float32 [2, 8, 96, 2048], P(None, 'band', None, 'ga')
- density: float32 [96, 9216], P('ga', 'band')
Inputs may be any that keep to these rules, and one draw needn't show every extreme that they name: `stick_xy`: 2048 distinct columns, each with both frequencies f(y) and f(x) in -(32) to 31. `dij`: each of the 2 matrices is symmetric positive definite with diagonal at least 0.5.
All inputs are finite; a program needn't handle non-finite values.
Results may differ from a plain program's by a relative error of at most 0.0003.
Values may be sent and summed in bfloat16 or wider, within the bound.
No kernel may reach another device: no remote copies, remote signals or barrier semaphores. Data moves between devices by JAX's collectives and lax.ppermute only.
A program may use at most 128 MiB of HBM per device.

v0:
```python
import math

import jax
import jax.numpy as jnp
from jax import lax
from jax.sharding import PartitionSpec as P

GRID = 96
STICKS = 2048
ITERS = 2


highest = lax.Precision.HIGHEST


def dft_table(length, sign):
    index = jnp.arange(length, dtype=jnp.int32)
    phase = index[:, None] * index[None, :] % length
    angle = phase.astype(jnp.float32) * (2.0 * math.pi / length)
    factor = 1.0 / math.sqrt(length)
    return (jnp.cos(angle) * factor, sign * jnp.sin(angle) * factor)


def square_table(sign):
    radius_cells = GRID // 3
    index = jnp.arange(GRID, dtype=jnp.int32)
    freqs = (jnp.arange(2 * radius_cells, dtype=jnp.int32) - radius_cells) % GRID
    phase = index[:, None] * freqs[None, :] % GRID
    angle = phase.astype(jnp.float32) * (2.0 * math.pi / GRID)
    factor = 1.0 / math.sqrt(GRID)
    return (jnp.cos(angle) * factor, sign * jnp.sin(angle) * factor)


def complex_apply(table, data, form):
    real_part = jnp.einsum(form, table[0], data[0], precision=highest) - jnp.einsum(
        form, table[1], data[1], precision=highest
    )
    imag_part = jnp.einsum(form, table[0], data[1], precision=highest) + jnp.einsum(
        form, table[1], data[0], precision=highest
    )
    return jnp.stack([real_part, imag_part])


def frequency(index):
    return (index + GRID // 2) % GRID - GRID // 2


def intersects_of(occupied, products):
    inv_norm = 1.0 / (2.0 * GRID * STICKS)
    real_part = jnp.einsum("cmzs,cnzs->mn", occupied, products, precision=highest) * inv_norm
    imag_part = (
        jnp.einsum("mzs,nzs->mn", occupied[0], products[1], precision=highest)
        - jnp.einsum("mzs,nzs->mn", occupied[1], products[0], precision=highest)
    ) * inv_norm
    return jnp.stack([real_part, imag_part])


def correction(intersect, occupied):
    real_part = jnp.einsum(
        "mn,mzs->nzs", intersect[0], occupied[0], precision=highest
    ) - jnp.einsum("mn,mzs->nzs", intersect[1], occupied[1], precision=highest)
    imag_part = jnp.einsum(
        "mn,mzs->nzs", intersect[1], occupied[0], precision=highest
    ) + jnp.einsum("mn,mzs->nzs", intersect[0], occupied[1], precision=highest)
    return jnp.stack([real_part, imag_part])


def per_device(psi, vloc, dv, beta, dij, atom_type, stick_xy, band_shift):
    inverse = dft_table(GRID, 1.0)
    forward = dft_table(GRID, -1.0)
    square_inv = square_table(1.0)
    square_fwd = square_table(-1.0)
    radius_cells = GRID // 3
    side = 2 * radius_cells
    local_sticks = psi.shape[3]
    area = GRID * GRID
    band_count = psi.shape[1]
    atom_count = atom_type.shape[0]
    per_atom = dij.shape[1]
    slots = jnp.arange(side, dtype=jnp.int32)
    row_slot = frequency(stick_xy // GRID) + radius_cells
    col_slot = frequency(stick_xy % GRID) + radius_cells
    row_onehot = (row_slot[:, None] == slots[None, :]).astype(jnp.float32)
    col_onehot = (col_slot[:, None] == slots[None, :]).astype(jnp.float32)

    def fill_planes(piece):
        scaled = piece[..., None] * row_onehot
        square = jnp.einsum("cpbsy,sx->cpbyx", scaled, col_onehot, precision=highest)
        along_x = complex_apply(square_inv, square, "xk,pbyk->pbyx")
        along_y = complex_apply(square_inv, along_x, "yk,pbkx->pbyx")
        return along_y.reshape(piece.shape[:3] + (area,))

    def to_real(coef):
        along_z = complex_apply(inverse, coef, "kz,bzs->kbs")
        return fill_planes(lax.all_to_all(along_z, "ga", split_axis=1, concat_axis=3, tiled=True))

    def z_forward(piece):
        return complex_apply(forward, piece, "kz,zbs->bks")

    def to_sticks(field):
        shaped = field.reshape(field.shape[:3] + (GRID, GRID))
        along_x = complex_apply(square_fwd, shaped, "xk,pbyx->pbyk")
        square = complex_apply(square_fwd, along_x, "yk,pbyx->pbkx")
        by_row = jnp.einsum("cpbyx,sx->cpbys", square, col_onehot, precision=highest)
        columns = jnp.sum(by_row * row_onehot.T, axis=3)
        return z_forward(lax.all_to_all(columns, "ga", split_axis=3, concat_axis=1, tiled=True))

    start = lax.axis_index("ga") * local_sticks
    own_xy = lax.dynamic_slice_in_dim(stick_xy, start, local_sticks)
    freq_z = frequency(jnp.arange(GRID, dtype=jnp.int32))
    summed = (
        freq_z[:, None] ** 2
        + (frequency(own_xy // GRID) ** 2 + frequency(own_xy % GRID) ** 2)[None, :]
    )
    kinetic = summed.astype(jnp.float32) * (4.0 / (GRID * GRID))
    diagonal = (kinetic[None] + band_shift[:, None, None])[None]
    vloc_wide = vloc[None, :, None, :]
    occupied = psi.astype(jnp.float32)
    psi_real = to_real(occupied)
    image_dv = to_sticks(dv[None, :, None, :] * psi_real)
    gathered = lax.all_gather(psi, "band", axis=1, tiled=True).astype(jnp.float32)
    intersect = lax.psum(intersects_of(gathered, image_dv), "ga")
    rhs = correction(intersect, gathered) - image_dv
    onehot = (atom_type[:, None] == jnp.arange(dij.shape[0], dtype=jnp.int32)[None, :]).astype(
        jnp.float32
    )
    selected = jnp.einsum("at,tij->aij", onehot, dij, precision=highest)

    def norm_of(vector):
        return lax.psum(jnp.sum(vector * vector, axis=(0, 2, 3)), "ga")

    solution = jnp.zeros_like(rhs)
    residual = rhs
    direction = rhs
    norm_now = norm_of(rhs)
    for iteration in range(ITERS):
        vector_real = to_real(direction)
        local = to_sticks(vloc_wide * vector_real)
        project_real_part = jnp.einsum(
            "jzs,bzs->jb", beta[0], direction[0], precision=highest
        ) + jnp.einsum("jzs,bzs->jb", beta[1], direction[1], precision=highest)
        project_imag_part = jnp.einsum(
            "jzs,bzs->jb", beta[0], direction[1], precision=highest
        ) - jnp.einsum("jzs,bzs->jb", beta[1], direction[0], precision=highest)
        projected_part = jnp.stack([project_real_part, project_imag_part])
        local_part = jnp.sum(diagonal * direction * direction, axis=(0, 2, 3)) + jnp.sum(
            vloc_wide * vector_real * vector_real, axis=(0, 1, 3)
        )
        apply_projected, local_total = lax.psum((projected_part, local_part), "ga")
        couple_shaped = apply_projected.reshape(2, atom_count, per_atom, band_count)
        apply_coupled = jnp.einsum(
            "aij,cajb->caib", selected, couple_shaped, precision=highest
        ).reshape(apply_projected.shape)
        real_part = jnp.einsum(
            "jzs,jb->bzs", beta[0], apply_coupled[0], precision=highest
        ) - jnp.einsum("jzs,jb->bzs", beta[1], apply_coupled[1], precision=highest)
        imag_part = jnp.einsum(
            "jzs,jb->bzs", beta[0], apply_coupled[1], precision=highest
        ) + jnp.einsum("jzs,jb->bzs", beta[1], apply_coupled[0], precision=highest)
        image_now = diagonal * direction + local + jnp.stack([real_part, imag_part])
        curvature_sum = local_total + jnp.sum(apply_projected * apply_coupled, axis=(0, 1))
        image_now, curvature_sum, direction_real = (image_now, curvature_sum, vector_real)
        alpha = (norm_now / curvature_sum)[None, :, None, None]
        solution = solution + alpha * direction
        residual = residual - alpha * image_now
        if iteration + 1 < ITERS:
            norm_next = norm_of(residual)
            direction = residual + (norm_next / norm_now)[None, :, None, None] * direction
            norm_now = norm_next
    response_real = to_real(solution)
    contribution = 4.0 * jnp.sum(psi_real * response_real, axis=(0, 2))
    density = lax.psum_scatter(contribution, "band", scatter_dimension=1, tiled=True)
    return (solution, density)


def solution(mesh):
    placed = (
        P(None, "band", None, "ga"),
        P("ga", None),
        P("ga", None),
        P(None, None, None, "ga"),
        P(),
        P(),
        P(),
        P("band"),
    )
    return jax.shard_map(
        per_device,
        mesh=mesh,
        in_specs=placed,
        out_specs=(P(None, "band", None, "ga"), P("ga", "band")),
        check_vma=False,
    )
```

profile of v0, /device:TPU:0, one launch (start us, length us, event | category | flops | bytes accessed | tf_op | source)
XLA Modules:
  0.0 725.8 jit_solution(4898030993601098272)
XLA Ops:
  13.5 5.2 all-to-all-start
  19.9 19.6 %fusion.744 = (f32[1,128,96,256]{3,2,1,0:T(8,128)}, f32[1,128,96,256]{3,2,1,0:T(8,128)}) fusion(f32[2,128,96,256]{3,2,1,0:T(8,128)} %param.11), kind=kLoop, calls=%fused_computation.792 | loop fusion | bytes 50331648 | tf_op jit(solution)/shard_map/slice | solution.py:140
  39.6 20.3 %all_gather.3 = bf16[2,8,96,256]{3,2,0,1:T(8,128)(2,1)} all-gather(bf16[2,2,96,256]{3,2,0,1:T(8,128)(2,1)S(1)} %copy.186), channel_id=1, replica_groups=mesh['ga'=8,'band'=4] {'band'}, dimensions={1}, use_global_device_ids=true | all-gather | bytes 983040 | tf_op jit(solution)/shard_map/all_gather | solution.py:121
  60.3 12.9 %fusion.6 = f32[2,12,2,64,64]{4,3,2,1,0:T(8,128)S(1)} fusion(f32[2048,64]{0,1:T(8,128)S(1)} %fusion.87, f32[2,12,2,2048]{3,2,1,0:T(2,128)S(1)} %mul.975, s32[2048]{0:T(1024)S(1)} %get-tuple-element.32), kind=kOutput, calls=%fused_computation.8 | convolution fusion | flops 4838260736 | bytes 1712128 | tf_op jit(solution)/shard_map/cpbsy,sx->cpbyx/dot_general | solution.py:88
  84.8 3.3 stack.156
  98.7 3.8 fusion.258
  102.5 3.1 squeeze.69
  105.6 4.3 fusion.254
  112.7 3.0 convolution_add_fusion.11
  119.7 12.6 %multiply_reduce_fusion.1 = f32[2,12,2,2048]{3,2,1,0:T(2,128)} fusion(f32[64,2048]{1,0:T(8,128)S(1)} %copy-done.25, f32[1,12,2,64,64]{3,4,2,1,0:T(8,128)S(1)} %fusion.46, f32[1,12,2,64,64]{3,4,2,1,0:T(8,128)S(1)} %fusion.47, s32[2048]{0:T(1024)S(1)} %get-tuple-element.32), kind=kOutput, calls=%fused_computation.7 | convolution fusion | flops 4844650496 | bytes 1712128 | tf_op jit(solution)/shard_map/cpbyx,sx->cpbys/dot_general | solution.py:104
  132.3 5.9 copy.178
  138.2 9.0 %reshape.198 = f32[8,1,12288]{2,1,0:T(1,128)} reshape(f32[2048,2,2,12]{3,2,1,0:T(2,128)} %bitcast.564) | data formatting | bytes 786432
  147.2 4.8 all-to-all-start.1
  154.6 5.6 all-to-all-done.1
  162.4 8.7 %reshape.199 = f32[2048,2,2,12]{3,2,1,0:T(2,128)} reshape(f32[8,12288]{1,0:T(8,128)S(1)} %reduce) | data formatting | bytes 786432
  171.1 3.6 copy.254
  181.8 11.9 %psum.49 = f32[2,8,2]{1,2,0:T(2,128)S(1)} all-reduce(f32[2,8,2]{1,2,0:T(2,128)S(1)} %pad_maximum_fusion.5), channel_id=1, replica_groups=mesh['ga'=8,'band'=4] {'ga'}, use_global_device_ids=true, to_apply=%region_1.2 | all-reduce | flops 32 | bytes 256 | tf_op jit(solution)/shard_map/psum | solution.py:122
  199.7 3.6 all-to-all-start.2
  203.3 19.8 %fusion.59 = f32[2,128]{1,0:T(2,128)S(1)} fusion(f32[1,128,96,256]{3,2,1,0:T(8,128)} %get-tuple-element.15, f32[2,96,256]{2,1,0:T(8,128)S(1)} %get-tuple-element.27), kind=kOutput, calls=%fused_computation.105 | convolution fusion | flops 75497472 | bytes 12780544 | tf_op jit(solution)/shard_map/jzs,bzs->jb/dot_general | solution.py:144
  223.1 20.0 %fusion.58 = f32[2,128]{1,0:T(2,128)S(1)} fusion(f32[1,128,96,256]{3,2,1,0:T(8,128)} %get-tuple-element.15, f32[2,96,256]{2,1,0:T(8,128)S(1)} %get-tuple-element.26), kind=kOutput, calls=%fused_computation.104 | convolution fusion | flops 75497472 | bytes 12780544 | tf_op jit(solution)/shard_map/jzs,bzs->jb/dot_general | solution.py:141
  243.2 15.3 %fusion.76 = f32[1,128,2]{1,2,0:T(2,128)S(1)} fusion(f32[2,128]{1,0:T(2,128)S(1)} %fusion.59, f32[1,128,96,256]{3,2,1,0:T(8,128)S(1)} %bitcast.561, f32[2,96,256]{2,1,0:T(8,128)S(1)} %get-tuple-element.26), kind=kOutput, calls=%fused_computation.125 | convolution fusion | flops 75497728 | bytes 12781568 | tf_op jit(solution)/shard_map/jzs,bzs->jb/dot_general | solution.py:142
  258.5 15.2 %fusion.78 = f32[1,128,2]{1,2,0:T(2,128)S(1)} fusion(f32[2,128]{1,0:T(2,128)S(1)} %fusion.58, f32[1,128,96,256]{3,2,1,0:T(8,128)S(1)} %bitcast.561, f32[2,96,256]{2,1,0:T(8,128)S(1)} %get-tuple-element.27), kind=kOutput, calls=%fused_computation.127 | convolution fusion | flops 75497728 | bytes 12781568 | tf_op jit(solution)/shard_map/jzs,bzs->jb/dot_general | solution.py:139
  274.7 14.0 %fusion.4 = f32[2,12,2,64,64]{4,3,2,1,0:T(8,128)S(1)} fusion(f32[2,12,2,2048]{3,2,1,0:T(2,128)S(1)} %mul.1004, f32[2048,64]{0,1:T(8,128)} %copy-done.23, s32[2048]{0:T(1024)S(1)} %get-tuple-element.32), kind=kOutput, calls=%fused_computation.5 | convolution fusion | flops 4838260736 | bytes 1712128 | tf_op jit(solution)/shard_map/cpbsy,sx->cpbyx/dot_general | solution.py:88
  294.7 3.2 fusion.246
  297.9 3.1 fusion.41
  303.6 3.3 stack.174
  307.0 4.7 fusion.40
  317.0 3.1 broadcast_multiply_fusion
  320.2 15.0 %all-reduce.1 = (f32[2,128,2]{1,2,0:T(2,128)S(1)}, f32[2]{0:T(128)}, f32[2]{0:T(128)}) all-reduce(f32[2,128,2]{1,2,0:T(2,128)S(1)} %copy-done.29, f32[2]{0:T(128)S(1)} %copy-done.32, f32[2]{0:T(128)S(1)} %add.563), channel_id=1, replica_groups=mesh['ga'=8,'band'=4] {'ga'}, use_global_device_ids=true, to_apply=%region_7.8 | all-reduce | flops 516 | bytes 4128 | tf_op jit(solution)/shard_map/psum | solution.py:149
  336.5 17.9 %fusion.24 = f32[2,96,256]{2,0,1:T(2,128)} fusion(f32[128,2,1]{0,1,2:T(2,128)S(1)} %reshape.189, f32[1,128,96,256]{3,2,1,0:T(8,128)} %get-tuple-element.15), kind=kOutput, calls=%fused_computation.28 | convolution fusion | flops 75497472 | bytes 12780544 | tf_op jit(solution)/shard_map/jzs,jb->bzs/dot_general | solution.py:159
  354.4 17.9 %fusion.19 = f32[2,96,256]{2,0,1:T(2,128)} fusion(f32[128,2,1]{0,1,2:T(2,128)S(1)} %reshape.189, f32[1,128,96,256]{3,2,1,0:T(8,128)} %get-tuple-element.14), kind=kOutput, calls=%fused_computation.23 | convolution fusion | flops 75497472 | bytes 12780544 | tf_op jit(solution)/shard_map/jzs,jb->bzs/dot_general | solution.py:154
  372.4 18.3 %fusion.18 = f32[2,96,256]{2,0,1:T(2,128)} fusion(f32[128,2,1]{0,1,2:T(2,128)S(1)} %reshape.190, f32[1,128,96,256]{3,2,1,0:T(8,128)} %get-tuple-element.14), kind=kOutput, calls=%fused_computation.22 | convolution fusion | flops 75497472 | bytes 12780544 | tf_op jit(solution)/shard_map/jzs,jb->bzs/dot_general | solution.py:157
  390.7 18.2 %fusion.25 = f32[2,96,256]{2,0,1:T(2,128)} fusion(f32[128,2,1]{0,1,2:T(2,128)S(1)} %reshape.190, f32[1,128,96,256]{3,2,1,0:T(8,128)} %get-tuple-element.15), kind=kOutput, calls=%fused_computation.29 | convolution fusion | flops 75497472 | bytes 12780544 | tf_op jit(solution)/shard_map/jzs,jb->bzs/dot_general | solution.py:156
  412.4 3.8 fusion.244
  416.1 3.1 squeeze.165
  419.2 4.3 fusion.240
  433.5 12.1 %multiply_reduce_fusion = f32[2,12,2,2048]{3,2,1,0:T(2,128)S(1)} fusion(f32[64,2048]{1,0:T(8,128)S(1)} %copy-done.26, f32[1,12,2,64,64]{3,4,2,1,0:T(8,128)S(1)} %fusion.44, f32[1,12,2,64,64]{3,4,2,1,0:T(8,128)S(1)} %fusion.45, s32[2048]{0:T(1024)S(1)} %get-tuple-element.32), kind=kOutput, calls=%fused_computation.4 | convolution fusion | flops 4844650496 | bytes 1712128 | tf_op jit(solution)/shard_map/cpbyx,sx->cpbys/dot_general | solution.py:104
  445.6 4.5 copy.213
  450.1 9.1 %reshape.200 = f32[8,1,12288]{2,1,0:T(1,128)} reshape(f32[2048,2,2,12]{3,2,1,0:T(2,128)} %bitcast.566) | data formatting | bytes 786432
  459.1 4.0 all-to-all-start.3
  465.1 6.3 all-to-all-done.3
  472.9 8.7 %reshape.201 = f32[2048,2,2,12]{3,2,1,0:T(2,128)} reshape(f32[8,12288]{1,0:T(8,128)S(1)} %reduce.1) | data formatting | bytes 786432
  481.6 3.6 copy.258
  487.9 11.8 %psum.53 = f32[2]{0:T(128)S(1)} all-reduce(f32[2]{0:T(128)S(1)} %get-tuple-element.11), channel_id=1, replica_groups=mesh['ga'=8,'band'=4] {'ga'}, use_global_device_ids=true, to_apply=%region_11.12 | all-reduce | flops 2 | bytes 16 | tf_op jit(solution)/shard_map/psum | solution.py:130
  504.3 3.5 all-to-all-start.4
  507.9 20.0 %fusion.60 = f32[2,128]{1,0:T(2,128)S(1)} fusion(f32[1,128,96,256]{3,2,1,0:T(8,128)} %get-tuple-element.15, f32[2,96,256]{2,1,0:T(8,128)S(1)} %get-tuple-element.22), kind=kOutput, calls=%fused_computation.106 | convolution fusion | flops 75497472 | bytes 12780544 | tf_op jit(solution)/shard_map/jzs,bzs->jb/dot_general | solution.py:141
  527.8 20.0 %fusion.61 = f32[2,128]{1,0:T(2,128)S(1)} fusion(f32[1,128,96,256]{3,2,1,0:T(8,128)} %get-tuple-element.15, f32[2,96,256]{2,1,0:T(8,128)S(1)} %get-tuple-element.23), kind=kOutput, calls=%fused_computation.107 | convolution fusion | flops 75497472 | bytes 12780544 | tf_op jit(solution)/shard_map/jzs,bzs->jb/dot_general | solution.py:144
  547.9 15.4 %fusion.74 = f32[1,128,2]{1,2,0:T(2,128)S(1)} fusion(f32[2,128]{1,0:T(2,128)S(1)} %fusion.60, f32[1,128,96,256]{3,2,1,0:T(8,128)S(1)} %bitcast.563, f32[2,96,256]{2,1,0:T(8,128)S(1)} %get-tuple-element.23), kind=kOutput, calls=%fused_computation.123 | convolution fusion | flops 75497728 | bytes 12781568 | tf_op jit(solution)/shard_map/jzs,bzs->jb/dot_general | solution.py:139
  563.3 15.0 %fusion.72 = f32[1,128,2]{1,2,0:T(2,128)S(1)} fusion(f32[2,128]{1,0:T(2,128)S(1)} %fusion.61, f32[1,128,96,256]{3,2,1,0:T(8,128)S(1)} %bitcast.563, f32[2,96,256]{2,1,0:T(8,128)S(1)} %get-tuple-element.22), kind=kOutput, calls=%fused_computation.121 | convolution fusion | flops 75497728 | bytes 12781568 | tf_op jit(solution)/shard_map/jzs,bzs->jb/dot_general | solution.py:142
  578.9 14.0 %fusion.2 = f32[2,12,2,64,64]{4,3,2,1,0:T(8,128)S(1)} fusion(f32[2,12,2,2048]{3,2,1,0:T(2,128)S(1)} %mul.1019, f32[2048,64]{0,1:T(8,128)} %copy-done.23, s32[2048]{0:T(1024)S(1)} %get-tuple-element.32), kind=kOutput, calls=%fused_computation.2 | convolution fusion | flops 4838260736 | bytes 1712128 | tf_op jit(solution)/shard_map/cpbsy,sx->cpbyx/dot_general | solution.py:88
  598.9 3.1 fusion.232
  602.0 3.1 fusion.39
  607.8 3.3 stack.192
  611.1 4.6 fusion.38
  618.4 3.4 stack.193
  625.1 14.3 %all-reduce = (f32[2]{0:T(128)S(1)}, f32[2,128,2]{1,2,0:T(2,128)S(1)}) all-reduce(f32[2]{0:T(128)S(1)} %add.580, f32[2,128,2]{1,2,0:T(2,128)S(1)} %pad_maximum_fusion.7), channel_id=1, replica_groups=mesh['ga'=8,'band'=4] {'ga'}, use_global_device_ids=true, to_apply=%region_14.15 | all-reduce | flops 514 | bytes 4112 | tf_op jit(solution)/shard_map/psum | solution.py:149
  642.8 10.7 %all_to_all.90 = f32[2,96,2,256]{3,2,0,1:T(2,128)S(1)} all-to-all(f32[2,96,2,256]{3,2,0,1:T(2,128)S(1)} %copy.239), channel_id=1, replica_groups=mesh['ga'=8,'band'=4] {'ga'}, dimensions={1} | all-to-all | bytes 786432 | tf_op jit(solution)/shard_map/all_to_all | solution.py:95
  654.0 12.9 %fusion = f32[2,12,2,64,64]{4,3,2,1,0:T(8,128)S(1)} fusion(f32[2,12,2,2048]{3,2,1,0:T(2,128)S(1)} %mul.1027, f32[2048,64]{0,1:T(8,128)S(1)} %copy-done.24, s32[2048]{0:T(1024)S(1)} %get-tuple-element.32), kind=kOutput, calls=%fused_computation | convolution fusion | flops 4838260736 | bytes 1712128 | tf_op jit(solution)/shard_map/cpbsy,sx->cpbyx/dot_general | solution.py:88
  672.9 3.1 fusion.226
  676.0 3.1 fusion.37
  681.8 3.3 stack.201
  685.1 4.7 fusion.36
  693.5 3.9 fusion.29
  698.4 20.1 %reduce-scatter.2.cloned.1.call-done = f32[12,2304]{1,0:T(8,128)} async-done(((f32[12,9216]{1,0:T(8,128)}), f32[12,2304]{1,0:T(8,128)}) %reduce-scatter.2.cloned.1.call-update) | async-done | bytes 110608 | tf_op jit(solution)/shard_map/reduce_scatter | solution.py:172
  (256 shorter events, 127.1 us)
Async XLA Ops:
  7.2 144.8 %copy-start = (f32[2,4,4]{2,1,0:T(4,128)S(1)}, f32[2,4,4]{2,1,0:T(4,128)}, u32[]{:S(2)}) copy-start(f32[2,4,4]{2,1,0:T(4,128)} %param.12) | copy-start | bytes 388
  9.8 8.9 %copy-start.28 = (s32[2048]{0:T(1024)S(1)}, s32[2048]{0:T(1024)}, u32[]{:S(2)}) copy-start(s32[2048]{0:T(1024)} %param.14) | copy-start | bytes 24580
  13.5 46.3 %all-to-all-start = ((f32[2,96,2,256]{3,2,0,1:T(2,128)}), f32[2,96,2,256]{3,2,0,1:T(2,128)S(1)}, u32[]{:S(2)}, u32[]{:S(2)}) async-start(f32[2,96,2,256]{3,2,0,1:T(2,128)} %copy.172), calls=%async_computation | async-start | bytes 786432 | tf_op jit(solution)/shard_map/all_to_all | solution.py:95
  18.8 41.5 %copy-start.23 = (f32[2048,64]{0,1:T(8,128)}, f32[2048,64]{0,1:T(8,128)S(1)}, u32[]{:S(2)}) copy-start(f32[2048,64]{0,1:T(8,128)S(1)} %fusion.87) | copy-start | bytes 1572868
  19.9 19.7 %copy-start.16 = (bf16[2,2,96,256]{3,2,1,0:T(8,128)(2,1)S(1)}, bf16[2,2,96,256]{3,2,1,0:T(8,128)(2,1)}, u32[]{:S(2)}) copy-start(bf16[2,2,96,256]{3,2,1,0:T(8,128)(2,1)} %param.8) | copy-start | bytes 589828
  91.0 2.2 copy-start.5
  93.2 1.2 copy-start.7
  93.2 1.3 copy-start.22
  105.6 4.3 copy-start.2
  105.6 4.3 copy-start.12
  118.7 1.0 copy-start.25
  138.2 13.8 %copy-start.38 = (s32[32]{0:T(128)S(1)}, s32[32]{0:T(128)}, u32[]{:S(2)}) copy-start(s32[32]{0:T(128)} %param.13) | copy-start | bytes 388
  147.2 7.3 %copy-start.33 = (f32[2]{0:T(128)S(1)}, f32[2]{0:T(128)}, u32[]{:S(2)}) copy-start(f32[2]{0:T(128)} %param.15) | copy-start | bytes 28
  147.2 13.0 %all-to-all-start.1 = ((f32[8,1,12288]{2,1,0:T(1,128)}), f32[8,1,12288]{2,1,0:T(1,128)S(1)}, u32[]{:S(2)}, u32[]{:S(2)}) async-start(f32[8,1,12288]{2,1,0:T(1,128)} %reshape.198), calls=%async_computation.1 | async-start | bytes 786432 | tf_op jit(solution)/shard_map/all_to_all | solution.py:106
  174.8 2.3 copy-start.11
  199.7 74.5 %all-to-all-start.2 = ((f32[2,96,2,256]{3,2,0,1:T(2,128)}), f32[2,96,2,256]{3,2,0,1:T(2,128)S(1)}, u32[]{:S(2)}, u32[]{:S(2)}) async-start(f32[2,96,2,256]{3,2,0,1:T(2,128)} %copy.197), calls=%async_computation.2 | async-start | bytes 786432 | tf_op jit(solution)/shard_map/all_to_all | solution.py:95
  203.3 39.8 %slice-start = ((s8[12582912]{0:T(1024)(128)(4,1)}), s8[4194304]{0:T(1024)(128)(4,1)S(1)}, s32[]{:S(2)}) async-start(s8[12582912]{0:T(1024)(128)(4,1)} %bitcast.560), calls=%async_computation.8 | async-start | bytes 8388608
  203.3 39.8 %slice-start.1 = ((s8[12582912]{0:T(1024)(128)(4,1)}), s8[4194304]{0:T(1024)(128)(4,1)S(1)}, s32[]{:S(2)}) async-start(s8[12582912]{0:T(1024)(128)(4,1)} %bitcast.560), calls=%async_computation.9 | async-start | bytes 8388608
  223.1 20.0 %slice-start.2 = ((s8[12582912]{0:T(1024)(128)(4,1)}), s8[4194304]{0:T(1024)(128)(4,1)S(1)}, s32[]{:S(2)}) async-start(s8[12582912]{0:T(1024)(128)(4,1)} %bitcast.560), calls=%async_computation.10 | async-start | bytes 8388608
  315.4 1.4 copy-start.8
  315.4 1.6 copy-start.14
  317.0 3.1 copy-start.34
  317.0 3.2 copy-start.29
  317.0 3.2 copy-start.32
  317.0 18.3 %copy-start.20 = (f32[32,4,4,1]{2,1,3,0:T(4,128)S(1)}, f32[32,4,4,1]{2,1,3,0:T(4,128)}, u32[]{:S(2)}) copy-start(f32[32,4,4,1]{2,1,3,0:T(4,128)} %copy.250) | copy-start | bytes 6148
  390.7 18.2 %copy-start.4 = (f32[2,12,2,9216]{3,2,1,0:T(2,128)S(1)}, f32[2,12,2,9216]{3,2,1,0:T(2,128)}, u32[]{:S(2)}) copy-start(f32[2,12,2,9216]{3,2,1,0:T(2,128)} %get-tuple-element.16) | copy-start | bytes 5308420
  419.2 4.3 copy-start.3
  419.2 4.3 copy-start.13
  432.4 1.0 copy-start.26
  450.1 13.1 %copy-start.27 = (f32[2,32,4,2]{2,1,3,0:T(8,128)S(1)}, f32[2,32,4,2]{2,1,3,0:T(8,128)}, u32[]{:S(2)}) copy-start(f32[2,32,4,2]{2,1,3,0:T(8,128)} %copy.211) | copy-start | bytes 6148
  450.1 13.3 %copy-start.18 = (f32[2,96,256]{2,0,1:T(2,128)S(1)}, f32[2,96,256]{2,0,1:T(2,128)}, u32[]{:S(2)}) copy-start(f32[2,96,256]{2,0,1:T(2,128)} %fusion.24) | copy-start | bytes 589828
  450.1 13.3 %copy-start.19 = (f32[2,96,256]{2,0,1:T(2,128)S(1)}, f32[2,96,256]{2,0,1:T(2,128)}, u32[]{:S(2)}) copy-start(f32[2,96,256]{2,0,1:T(2,128)} %fusion.18) | copy-start | bytes 589828
  459.1 5.0 copy-start.17
  459.1 12.2 %all-to-all-start.3 = ((f32[8,1,12288]{2,1,0:T(1,128)}), f32[8,1,12288]{2,1,0:T(1,128)S(1)}, u32[]{:S(2)}, u32[]{:S(2)}) async-start(f32[8,1,12288]{2,1,0:T(1,128)} %reshape.200), calls=%async_computation.3 | async-start | bytes 786432 | tf_op jit(solution)/shard_map/all_to_all | solution.py:106
  464.1 23.5 %copy-start.30 = (f32[2]{0:T(128)}, f32[2]{0:T(128)S(1)}, u32[]{:S(2)}) copy-start(f32[2]{0:T(128)S(1)} %add_divide_fusion.1) | copy-start | bytes 28
  499.7 0.6 copy-start.36
  504.3 74.0 %all-to-all-start.4 = ((f32[2,96,2,256]{3,2,0,1:T(2,128)}), f32[2,96,2,256]{3,2,0,1:T(2,128)S(1)}, u32[]{:S(2)}, u32[]{:S(2)}) async-start(f32[2,96,2,256]{3,2,0,1:T(2,128)} %copy.227), calls=%async_computation.4 | async-start | bytes 786432 | tf_op jit(solution)/shard_map/all_to_all | solution.py:95
  507.8 210.7 %reduce-scatter.2.cloned.1.call-start = ((), (), s32[]{:S(2)}) async-start(), calls=%async_computation.7 | async-start | bytes 737280 | tf_op jit(solution)/shard_map/reduce_scatter | solution.py:172
  507.9 40.0 %slice-start.3 = ((s8[12582912]{0:T(1024)(128)(4,1)}), s8[4194304]{0:T(1024)(128)(4,1)S(1)}, s32[]{:S(2)}) async-start(s8[12582912]{0:T(1024)(128)(4,1)} %bitcast.562), calls=%async_computation.11 | async-start | bytes 8388608
  507.9 40.0 %slice-start.4 = ((s8[12582912]{0:T(1024)(128)(4,1)}), s8[4194304]{0:T(1024)(128)(4,1)S(1)}, s32[]{:S(2)}) async-start(s8[12582912]{0:T(1024)(128)(4,1)} %bitcast.562), calls=%async_computation.12 | async-start | bytes 8388608
  527.8 20.0 %slice-start.5 = ((s8[12582912]{0:T(1024)(128)(4,1)}), s8[4194304]{0:T(1024)(128)(4,1)S(1)}, s32[]{:S(2)}) async-start(s8[12582912]{0:T(1024)(128)(4,1)} %bitcast.562), calls=%async_computation.13 | async-start | bytes 8388608
  618.4 3.4 copy-start.6
  621.8 1.2 copy-start.9
  621.8 1.3 copy-start.15
  623.1 2.0 copy-start.35
  623.1 16.4 %copy-start.21 = (f32[32,4,4,1]{2,1,3,0:T(4,128)S(1)}, f32[32,4,4,1]{2,1,3,0:T(4,128)}, u32[]{:S(2)}) copy-start(f32[32,4,4,1]{2,1,3,0:T(4,128)} %copy.250) | copy-start | bytes 6148
  623.1 17.0 %copy-start.37 = (f32[2]{0:T(128)S(1)}, f32[2]{0:T(128)}, u32[]{:S(2)}) copy-start(f32[2]{0:T(128)} %copy-done.36) | copy-start | bytes 28
  623.1 17.1 %copy-start.31 = (f32[2]{0:T(128)S(1)}, f32[2]{0:T(128)}, u32[]{:S(2)}) copy-start(f32[2]{0:T(128)} %copy-done.30) | copy-start | bytes 28
  640.3 2.5 copy-start.10
  642.5 11.5 %copy-start.24 = (f32[2048,64]{0,1:T(8,128)S(1)}, f32[2048,64]{0,1:T(8,128)}, u32[]{:S(2)}) copy-start(f32[2048,64]{0,1:T(8,128)} %copy-done.23) | copy-start | bytes 1572868
  693.5 25.0 %copy-start.1 = (f32[2,4,4]{2,1,0:T(4,128)S(1)}, f32[2,4,4]{2,1,0:T(4,128)}, u32[]{:S(2)}) copy-start(f32[2,4,4]{2,1,0:T(4,128)} %param.12) | copy-start | bytes 388
Sparse Core Ops, SparseCore 0:
  698.5 19.9 reduce-scatter.1
where the time goes:
time: 735 us; the launch traced here: 726 us
  matrix products  414 us (56%)
  local copies, waits for them, and re-layouts  139 us (19%)
  blocking collectives  83.9 us (11%)
  waiting for transfers between devices  32.1 us (4%)
  starting transfers between devices  21.1 us (3%)
  other arithmetic  20.3 us (3%)
  between operations  15.8 us (2%)
    dot_general x4, matrix products, fill_planes(): jnp.einsum('cpbsy,sx->cpbyx', scaled, col_onehot, precision=highest)  53.8 us
    dot_general x2, matrix products, per_device(): jnp.einsum('jzs,bzs->jb', beta[1], direction[1], precision=highest)  40 us
    dot_general x2, matrix products, per_device(): jnp.einsum('jzs,bzs->jb', beta[1], direction[0], precision=highest)  39.8 us
    unnamed x98, local copies, waits for them, and re-layouts  39.6 us
    dot_general x18, matrix products, complex_apply(): jnp.einsum(form, table[1], data[0], precision=highest)  32.3 us
    dot_general x2, matrix products, per_device(): jnp.einsum('jzs,bzs->jb', beta[0], direction[0], precision=highest)  30.5 us
    dot_general x2, matrix products, per_device(): jnp.einsum('jzs,bzs->jb', beta[0], direction[1], precision=highest)  30.3 us
    dot_general x18, matrix products, complex_apply(): jnp.einsum(form, table[0], data[1], precision=highest)  29.8 us
  transfers between devices with their start and end apart: 6, of which 3 were waited for; matrix products, arithmetic and copies ran while one was open for 23% of the time, Pallas kernels for 0%

commit v1 on v0

v1 whole, which is shorter than its diff:
```python
import functools

import jax
import jax.numpy as jnp
import numpy as np
from jax import lax
from jax.experimental import pallas as pl
from jax.experimental.pallas import tpu as pltpu
from jax.sharding import PartitionSpec as P

GRID = 96
ITERS = 2
SIDE = 2 * (GRID // 3)
LANES = 128
f32 = jnp.float32
bf16 = jnp.bfloat16
highest = lax.Precision.HIGHEST


def split_const(table):
    table = np.asarray(table, np.float32)
    high = table.astype(jnp.bfloat16)
    low = (table - high.astype(np.float32)).astype(jnp.bfloat16)
    return high, low


def phases(rows, cols):
    angle = (np.outer(rows, cols) % GRID) * (2.0 * np.pi / GRID)
    return np.cos(angle) / np.sqrt(GRID), np.sin(angle) / np.sqrt(GRID)


def z_table(bands):
    cos, sin = phases(np.arange(GRID), np.arange(GRID))
    table = np.zeros((GRID, bands, 2, 2, bands, GRID))
    for b in range(bands):
        table[:, b, 0, 0, b] = cos
        table[:, b, 0, 1, b] = -sin
        table[:, b, 1, 0, b] = sin
        table[:, b, 1, 1, b] = cos
    return table.reshape(GRID * bands * 2, 2 * bands * GRID)


def square_freqs():
    return (np.arange(SIDE) - SIDE // 2) % GRID


def y_table():
    cos, sin = phases(np.arange(GRID), square_freqs())
    return np.block([[cos, -sin], [sin, cos]])


def x_table():
    cos, sin = phases(square_freqs(), np.arange(GRID))
    table = np.zeros((SIDE, 2 * LANES))
    table[:, :GRID] = cos
    table[:, LANES : LANES + GRID] = sin
    return table


def x_back_table():
    cos, sin = phases(np.arange(GRID), square_freqs())
    table = np.zeros((LANES, 4 * SIDE))
    table[:GRID] = np.concatenate([cos, cos, sin, sin], axis=1)
    return table


def split(x):
    high = x.astype(bf16)
    return high, (x - high.astype(f32)).astype(bf16)


def dot(a, b):
    return jnp.dot(a, b, preferred_element_type=f32)


def left(table_hi, table_lo, x):
    high, low = split(x)
    return dot(table_hi, high) + (dot(table_hi, low) + dot(table_lo, high))


def right(x, table_hi, table_lo):
    high, low = split(x)
    return dot(high, table_hi) + (dot(low, table_hi) + dot(high, table_lo))


def params(grid_dims=0):
    semantics = ("arbitrary",) * grid_dims if grid_dims else None
    return pltpu.CompilerParams(
        vmem_limit_bytes=56 * 1024 * 1024, dimension_semantics=semantics
    )


def z_inverse_kernel(coef, t_hi, t_lo, out):
    value = coef[...]
    out[...] = dot(t_hi[...], value) + dot(t_lo[...], value)


def z_inverse(coef, table):
    return pl.pallas_call(
        z_inverse_kernel,
        out_shape=jax.ShapeDtypeStruct(coef.shape, f32),
        compiler_params=params(),
        name="z_inverse",
    )(coef, *table)


def intersect_kernel(bands, recv, occ, b_hi, b_lo, image, parts):
    image[...] = left(b_hi[...], b_lo[...], recv[...])
    total = occ.shape[0] * bands
    sticks = recv.shape[1]

    def lanes(x):
        row = jnp.sum(x, axis=0, keepdims=True)
        return sum(row[:, k : k + LANES] for k in range(0, sticks, LANES))

    for n in range(bands):
        re = image[n * GRID : (n + 1) * GRID, :]
        im = image[(bands + n) * GRID : (bands + n + 1) * GRID, :]
        for m in range(total):
            group, own = m // bands, m % bands
            o_re = occ[group, 0, own].astype(f32)
            o_im = occ[group, 1, own].astype(f32)
            at = m * bands + n
            parts[at : at + 1, :] = lanes(o_re * re + o_im * im)
            at = at + total * bands
            parts[at : at + 1, :] = lanes(o_re * im - o_im * re)


def planes_kernel(mode, bands, recv, pot, row, col1, col2, xt_hi, xt_lo, yt_hi, yt_lo, yb_hi, yb_lo, xb_hi, xb_lo, *rest):
    groups, rows, sticks = recv.shape
    planes = rows // (2 * bands)
    count = planes * bands
    rest = list(rest)
    if mode == "next":
        first, psi_field, ratio = rest[:3]
        rest = rest[3:]
    if mode == "local":
        psi_field = rest[0]
        rest = rest[1:]
    spread = rest[-1]
    for g in range(groups):
        at = g * sticks
        mask = row[:, at : at + sticks]
        value = recv[g]
        high = value.astype(bf16).astype(f32)
        low = value - high
        for part, piece in enumerate((high, low)):
            for r in range(rows):
                to = (part * rows + r) * SIDE
                spread[to : to + SIDE, at : at + sticks] = (mask * piece[r : r + 1, :]).astype(bf16)
    both = dot(spread[...], col1[...])
    half = rows * SIDE
    square = both[:half] + both[half:]
    wide = right(square, xt_hi[...], xt_lo[...])
    fields = []
    for n in range(count):
        re = wide[(2 * n) * SIDE : (2 * n + 1) * SIDE]
        im = wide[(2 * n + 1) * SIDE : (2 * n + 2) * SIDE]
        fields.append(
            jnp.concatenate([re[:, :LANES] - im[:, LANES:], re[:, LANES:] + im[:, :LANES]], axis=0)
        )
    field = left(yt_hi[...], yt_lo[...], jnp.concatenate(fields, axis=1))
    if mode == "next":
        quad, dens = rest[:2]
    elif mode == "local":
        field_out, quad, dens, back = rest[:4]
        field_out[0] = field
    else:
        field_out, back = rest[:2]
        field_out[0] = field
    if mode != "dv":
        sums = [jnp.zeros((1, LANES), f32) for _ in range(bands)]
    products = []
    for n in range(count):
        p, b = n // bands, n % bands
        at = n * LANES
        re = field[:GRID, at : at + LANES]
        im = field[GRID:, at : at + LANES]
        v = pot[p]
        if mode == "next":
            re = re + ratio[b] * first[0, :GRID, at : at + LANES]
            im = im + ratio[b] * first[0, GRID:, at : at + LANES]
        v_re, v_im = v * re, v * im
        if mode != "dv":
            dens[p, b] = (
                psi_field[0, :GRID, at : at + LANES] * re + psi_field[0, GRID:, at : at + LANES] * im
            )
            sums[b] = sums[b] + jnp.sum(v_re * re + v_im * im, axis=0, keepdims=True)
        products.append(jnp.concatenate([v_re, v_im], axis=0))
    if mode != "dv":
        quad[0] = jnp.concatenate(sums, axis=0)
    if mode == "next":
        return
    columns = left(yb_hi[...], yb_lo[...], jnp.concatenate(products, axis=1))
    stacked = jnp.concatenate([columns[:, n * LANES : (n + 1) * LANES] for n in range(count)], axis=0)
    wide = right(stacked, xb_hi[...], xb_lo[...])
    squares = []
    for n in range(count):
        re = wide[(2 * n) * SIDE : (2 * n + 1) * SIDE]
        im = wide[(2 * n + 1) * SIDE : (2 * n + 2) * SIDE]
        squares += [re[:, :LANES] + im[:, LANES:], im[:, :LANES] - re[:, LANES:]]
    square = jnp.concatenate(squares, axis=0)
    high = square.astype(bf16).astype(f32)
    lane = lax.broadcasted_iota(jnp.int32, square.shape, 1)
    pair = jnp.where(lane < SIDE, high, square - high).astype(bf16)
    for g in range(groups):
        at = g * sticks
        mask = row[:, at : at + sticks]
        by_row = dot(pair, col2[:, at : at + sticks])
        for r in range(rows):
            back[g, r : r + 1, :] = jnp.sum(
                by_row[r * SIDE : (r + 1) * SIDE] * mask, axis=0, keepdims=True
            )


def planes_call(mode, recv, pot, maps, tables, groups, bands, extra=()):
    rows, sticks = recv.shape
    recv = recv.reshape(groups, rows // groups, sticks)
    local = recv.shape[1]
    planes = local // (2 * bands)
    step = max(1, 8 // (2 * bands))
    if planes % step:
        step = planes
    steps = planes // step
    width = step * bands * LANES
    whole = lambda a: pl.BlockSpec(a.shape, lambda i: (0,) * a.ndim)
    sticks_spec = pl.BlockSpec((groups, step * 2 * bands, sticks), lambda i: (0, i, 0))
    field_spec = pl.BlockSpec((1, 2 * GRID, width), lambda i: (i, 0, 0))
    field_shape = jax.ShapeDtypeStruct((steps, 2 * GRID, width), f32)
    quad_spec = pl.BlockSpec((1, bands, LANES), lambda i: (i, 0, 0))
    quad_shape = jax.ShapeDtypeStruct((steps, bands, LANES), f32)
    dens_spec = pl.BlockSpec((step, bands, GRID, LANES), lambda i: (i, 0, 0, 0))
    dens_shape = jax.ShapeDtypeStruct((planes, bands, GRID, LANES), f32)
    back_shape = jax.ShapeDtypeStruct(recv.shape, f32)
    in_specs = [sticks_spec, pl.BlockSpec((step, GRID, LANES), lambda i: (i, 0, 0))]
    in_specs += [whole(a) for a in maps] + [whole(a) for a in tables]
    if mode == "dv":
        out_specs, out_shape = [field_spec, sticks_spec], [field_shape, back_shape]
    elif mode == "local":
        in_specs += [field_spec]
        out_specs = [field_spec, quad_spec, dens_spec, sticks_spec]
        out_shape = [field_shape, quad_shape, dens_shape, back_shape]
    else:
        in_specs += [field_spec, field_spec, pl.BlockSpec(memory_space=pltpu.SMEM)]
        out_specs, out_shape = [quad_spec, dens_spec], [quad_shape, dens_shape]
    result = pl.pallas_call(
        functools.partial(planes_kernel, mode, bands),
        grid=(steps,),
        in_specs=in_specs,
        out_specs=out_specs,
        out_shape=out_shape,
        scratch_shapes=[pltpu.VMEM((2 * step * 2 * bands * SIDE, groups * sticks), bf16)],
        compiler_params=params(1),
        name="planes_" + mode,
    )(recv, pot, *maps, *tables, *extra)
    if mode != "next":
        result = list(result)
        result[-1] = result[-1].reshape(rows, sticks)
    return result


def project(beta, vector, bands, acc, chunk):
    count = beta.shape[1]

    def fold(x):
        parts = [x[k : k + 8, l : l + LANES] for k in range(0, x.shape[0], 8) for l in range(0, x.shape[1], LANES)]
        while len(parts) > 1:
            parts = [sum(parts[k : k + 2][1:], parts[k]) for k in range(0, len(parts), 2)]
        return parts[0]

    def body(k, carry):
        for u in range(chunk):
            j = k * chunk + u
            b_re, b_im = beta[0, j], beta[1, j]
            for b in range(bands):
                re, im = vector[0][b], vector[1][b]
                acc[j, b] += fold(b_re * re + b_im * im)
                acc[j, bands + b] += fold(b_re * im - b_im * re)
        return carry

    lax.fori_loop(0, count // chunk, body, 0)


def emit(acc, projected, vec, out, t_hi, t_lo):
    projected[...] = jnp.sum(acc[...], axis=2)
    out[...] = left(t_hi[...], t_lo[...], vec[...])


def tile_sums(x):
    row = jnp.sum(x, axis=0, keepdims=True)
    return sum(row[:, k : k + LANES] for k in range(0, x.shape[1], LANES))


def rhs_kernel(bands, parts, occ, image, diag, beta, t_hi, t_lo, vec_out, stats, projected, out, vec, acc):
    step = pl.program_id(0)
    last = pl.num_programs(0) - 1
    zt = image.shape[2]
    total = occ.shape[0] * bands

    @pl.when(step == 0)
    def _():
        acc[...] = jnp.zeros_like(acc)
        stats[...] = jnp.zeros_like(stats)

    vector = [[], []]
    for n in range(bands):
        re, im = -image[0, n], -image[1, n]
        for m in range(total):
            group, own = m // bands, m % bands
            o_re = occ[group, 0, own].astype(f32)
            o_im = occ[group, 1, own].astype(f32)
            at = m * bands + n
            i_re = parts[0, at]
            i_im = parts[0, at + total * bands]
            re = re + (o_re * i_re - o_im * i_im)
            im = im + (o_re * i_im + o_im * i_re)
        vector[0].append(re)
        vector[1].append(im)
    for n in range(bands):
        d = diag[n]
        sq = vector[0][n] * vector[0][n] + vector[1][n] * vector[1][n]
        stats[0, n : n + 1, :] += tile_sums(sq)
        stats[1, n : n + 1, :] += tile_sums(d * sq)
        for c in range(2):
            vec_out[c, n] = vector[c][n]
            vec[pl.ds((c * bands + n) * GRID + step * zt, zt), :] = vector[c][n]
    project(beta, vector, bands, acc, 4)

    @pl.when(step == last)
    def _():
        emit(acc, projected, vec, out, t_hi, t_lo)


def update_kernel(bands, coupled, alpha, recv, p0, diag, beta, b_hi, b_lo, t_hi, t_lo, vec_out, stats, projected, out, vec, local, acc):
    step = pl.program_id(0)
    last = pl.num_programs(0) - 1
    zt = p0.shape[2]

    @pl.when(step == 0)
    def _():
        acc[...] = jnp.zeros_like(acc)
        stats[...] = jnp.zeros_like(stats)
        local[...] = left(b_hi[...], b_lo[...], recv[...])

    first = []
    for c in range(2):
        for n in range(bands):
            at = pl.multiple_of((c * bands + n) * GRID + step * zt, 8)
            first.append(diag[n] * p0[c, n] + local[pl.ds(at, zt), :])

    def body(k, carry):
        for u in range(2):
            j = k * 2 + u
            b_re, b_im = beta[0, j], beta[1, j]
            new = [None] * (2 * bands)
            for n in range(bands):
                w_re, w_im = coupled[n, j], coupled[bands + n, j]
                new[n] = carry[n] + (b_re * w_re - b_im * w_im)
                new[bands + n] = carry[bands + n] + (b_re * w_im + b_im * w_re)
            carry = tuple(new)
        return carry

    image = lax.fori_loop(0, beta.shape[1] // 2, body, tuple(first))
    vector = [[], []]
    for c in range(2):
        for n in range(bands):
            value = p0[c, n] - alpha[n] * image[c * bands + n]
            vector[c].append(value)
            vec_out[c, n] = value
            at = pl.multiple_of((c * bands + n) * GRID + step * zt, 8)
            vec[pl.ds(at, zt), :] = value
    for n in range(bands):
        d = diag[n]
        sq = vector[0][n] * vector[0][n] + vector[1][n] * vector[1][n]
        cross = vector[0][n] * p0[0, n] + vector[1][n] * p0[1, n]
        stats[0, n : n + 1, :] += tile_sums(sq)
        stats[1, n : n + 1, :] += tile_sums(d * sq)
        stats[2, n : n + 1, :] += tile_sums(d * cross)
    project(beta, vector, bands, acc, 4)

    @pl.when(step == last)
    def _():
        emit(acc, projected, vec, out, t_hi, t_lo)


def frequency(index):
    return (index + GRID // 2) % GRID - GRID // 2


def per_device(psi, vloc, dv, beta, dij, atom_type, stick_xy, band_shift, *, groups):
    bands, sticks = psi.shape[1], psi.shape[3]
    nproj = beta.shape[1]
    planes = vloc.shape[0]
    all_sticks = stick_xy.shape[0]
    flat = (2 * bands * GRID, sticks)
    shaped = (2, bands, GRID, sticks)
    table = z_table(bands)
    t_inv = [jnp.asarray(a) for a in split_const(table)]
    t_fwd = [jnp.asarray(a) for a in split_const(table.T)]
    tables = []
    for item in (x_table(), y_table(), y_table().T, x_back_table()):
        tables += [jnp.asarray(a) for a in split_const(item)]
    slots = jnp.arange(SIDE, dtype=jnp.int32)
    row_slot = frequency(stick_xy // GRID) + SIDE // 2
    col_slot = frequency(stick_xy % GRID) + SIDE // 2
    row_hot = (slots[:, None] == row_slot[None, :]).astype(f32)
    col_hot = (col_slot[:, None] == slots[None, :]).astype(bf16)
    twice = jnp.arange(2 * SIDE, dtype=jnp.int32) % SIDE
    col_twice = (twice[:, None] == col_slot[None, :]).astype(bf16)
    maps = (row_hot, col_hot, col_twice)

    def grid_of(field):
        return jnp.pad(field.reshape(planes, GRID, GRID), ((0, 0), (0, 0), (0, LANES - GRID)))

    def swap(x):
        return lax.all_to_all(x, "ga", split_axis=0, concat_axis=0, tiled=True)

    start = lax.axis_index("ga") * sticks
    own_xy = lax.dynamic_slice_in_dim(stick_xy, start, sticks)
    freq_z = frequency(jnp.arange(GRID, dtype=jnp.int32))
    summed = (
        freq_z[:, None] ** 2
        + (frequency(own_xy // GRID) ** 2 + frequency(own_xy % GRID) ** 2)[None, :]
    )
    kinetic = summed.astype(f32) * (4.0 / (GRID * GRID))
    diag = kinetic[None] + band_shift[:, None, None]
    onehot = (atom_type[:, None] == jnp.arange(dij.shape[0], dtype=jnp.int32)[None, :]).astype(f32)
    selected = jnp.einsum("at,tij->aij", onehot, dij, precision=highest)

    def couple(projected):
        parts = projected.reshape(2 * bands, selected.shape[0], selected.shape[1])
        return jnp.einsum("aij,caj->cai", selected, parts, precision=highest).reshape(2 * bands, nproj)

    occ = lax.all_gather(psi, "band", axis=0)
    dv_grid, vloc_grid = grid_of(dv), grid_of(vloc)
    along = swap(z_inverse(psi.reshape(flat), t_inv))
    psi_field, back = planes_call("dv", along, dv_grid, maps, tables, groups, bands)
    pairs = 2 * occ.shape[0] * bands * bands
    image, parts = pl.pallas_call(
        functools.partial(intersect_kernel, bands),
        out_shape=[jax.ShapeDtypeStruct(flat, f32), jax.ShapeDtypeStruct((pairs, LANES), f32)],
        compiler_params=params(),
        name="intersects",
    )(swap(back), occ, *t_fwd)
    inv_norm = 1.0 / (2.0 * GRID * all_sticks)
    intersect = (lax.psum(jnp.sum(parts, axis=1), "ga") * inv_norm)[None]

    zt = 16
    steps = GRID // zt
    whole = lambda a: pl.BlockSpec(a.shape, lambda i: (0,) * a.ndim)
    smem = pl.BlockSpec(memory_space=pltpu.SMEM)
    vec_spec = pl.BlockSpec((2, bands, zt, sticks), lambda i: (0, 0, i, 0))
    occ_spec = pl.BlockSpec((occ.shape[0], 2, bands, zt, sticks), lambda i: (0, 0, 0, i, 0))
    diag_spec = pl.BlockSpec((bands, zt, sticks), lambda i: (0, i, 0))
    beta_spec = pl.BlockSpec((2, nproj, zt, sticks), lambda i: (0, 0, i, 0))
    stats_shape = jax.ShapeDtypeStruct((3, bands, LANES), f32)
    proj_shape = jax.ShapeDtypeStruct((nproj, 2 * bands, LANES), f32)
    flat_shape = jax.ShapeDtypeStruct(flat, f32)
    outs = [jax.ShapeDtypeStruct(shaped, f32), stats_shape, proj_shape, flat_shape]
    out_specs = [vec_spec, whole(stats_shape), whole(proj_shape), whole(flat_shape)]
    acc_scratch = pltpu.VMEM((nproj, 2 * bands, 8, LANES), f32)

    p0, stats0, proj0, along = pl.pallas_call(
        functools.partial(rhs_kernel, bands),
        grid=(steps,),
        in_specs=[smem, occ_spec, vec_spec, diag_spec, beta_spec, whole(t_inv[0]), whole(t_inv[1])],
        out_specs=out_specs,
        out_shape=outs,
        scratch_shapes=[pltpu.VMEM(flat, f32), acc_scratch],
        compiler_params=params(1),
        name="rhs",
    )(intersect, occ, image.reshape(shaped), diag, beta, *t_inv)
    p0_field, quad0, dens0, back = planes_call(
        "local", swap(along), vloc_grid, maps, tables, groups, bands, (psi_field,)
    )
    stats0, proj0, quad0 = lax.psum(
        (jnp.sum(stats0, axis=2), jnp.sum(proj0, axis=2).T, jnp.sum(quad0, axis=(0, 2))), "ga"
    )
    coupled0 = couple(proj0)

    def band_dot(a, b):
        return jnp.sum((a * b).reshape(2, bands, nproj), axis=(0, 2))

    rr0 = stats0[0]
    alpha0 = rr0 / (stats0[1] + quad0 + band_dot(proj0, coupled0))
    r1, stats1, proj1, along = pl.pallas_call(
        functools.partial(update_kernel, bands),
        grid=(steps,),
        in_specs=[smem, smem, whole(flat_shape), vec_spec, diag_spec, beta_spec]
        + [whole(t_inv[0])] * 4,
        out_specs=out_specs,
        out_shape=outs,
        scratch_shapes=[pltpu.VMEM(flat, f32), pltpu.VMEM(flat, f32), acc_scratch],
        compiler_params=params(1),
        name="update",
    )(coupled0, alpha0, swap(back), p0, diag, beta, *t_fwd, *t_inv)
    stats1, proj1 = lax.psum((jnp.sum(stats1, axis=2), jnp.sum(proj1, axis=2).T), "ga")
    ratio = stats1[0] / rr0
    quad1, dens1 = planes_call(
        "next", swap(along), vloc_grid, maps, tables, groups, bands, (p0_field, psi_field, ratio)
    )
    quad1 = lax.psum(jnp.sum(quad1, axis=(0, 2)), "ga")
    spread_ratio = jnp.tile(ratio, 2)[:, None]
    proj_p1 = proj1 + spread_ratio * proj0
    diag1 = stats1[1] + ratio * (2.0 * stats1[2] + ratio * stats0[1])
    alpha1 = stats1[0] / (diag1 + quad1 + band_dot(proj_p1, couple(proj_p1)))
    wide = lambda a: a[None, :, None, None]
    response = wide(alpha1) * r1 + wide(alpha0 + alpha1 * ratio) * p0
    contribution = 4.0 * jnp.sum(wide(alpha0) * dens0 + wide(alpha1) * dens1, axis=1)
    density = lax.psum_scatter(contribution, "band", scatter_dimension=1, tiled=True)
    return response, density[:, :, :GRID].reshape(planes, -1)


def solution(mesh):
    placed = (
        P(None, "band", None, "ga"),
        P("ga", None),
        P("ga", None),
        P(None, None, None, "ga"),
        P(),
        P(),
        P(),
        P("band"),
    )
    return jax.shard_map(
        functools.partial(per_device, groups=mesh.shape["ga"]),
        mesh=mesh,
        in_specs=placed,
        out_specs=(P(None, "band", None, "ga"), P("ga", "band")),
        check_vma=False,
    )
```

time: 735 us -> 297 us (0.40); the launches traced: 726 us -> 296 us
  matrix products: 414 us -> 0.91 us
  local copies, waits for them, and re-layouts: 139 us -> 9.02 us
  Pallas kernels: 0 us -> 125 us
  blocking collectives: 83.9 us -> 67.7 us
  waiting for transfers between devices: 32.1 us -> 44.6 us
    dot_general x99 -> x2, matrix products: 413 us -> 0.72 us  [couple(): jnp.einsum('aij,caj->cai', selected, parts, precision=highest)]
    pallas_call x0 -> x7, Pallas kernels: none -> 125 us  [the longest x3 80.4 us: planes_call(): pl.pallas_call(functools.partial(planes_kernel, mode, bands), grid=(steps...]
    unnamed x98 -> x40, local copies, waits for them, and re-layouts: 39.6 us -> 4.27 us
    another operation x15 -> x1, local copies, waits for them, and re-layouts: 26.9 us -> 0.01 us  [per_device(): spread_ratio = jnp.tile(ratio, 2)[:, None]]
    slice x12 -> x0, local copies, waits for them, and re-layouts: 22.9 us -> none  [the longest x1 19.6 us: per_device(): beta[0]]
    all_to_all x5, waiting for transfers between devices: 12 us -> 24.6 us  [swap(): return lax.all_to_all(x, 'ga', split_axis=0, concat_axis=0, tiled=True)]
    all_to_all x1 -> x0, blocking collectives: 10.7 us -> none  [to_real(): lax.all_to_all(along_z, 'ga', split_axis=1, concat_axis=3, tiled=True)]
    squeeze x8 -> x0, local copies, waits for them, and re-layouts: 10.5 us -> none  [the longest x4 6.28 us: complex_apply(): data[1]]
  transfers between devices with their start and end apart: 6 -> 6, of which waited for: 3 -> 5; matrix products, arithmetic and copies ran while one was open for 23% -> 3% of each run, Pallas kernels for 0% -> 0%
where the time goes in v1:
time: 297 us; the launch traced here: 296 us
  Pallas kernels  125 us (42%)
  blocking collectives  67.7 us (23%)
  waiting for transfers between devices  44.6 us (15%)
  starting transfers between devices  19.7 us (7%)
  between operations  14.4 us (5%)
  other arithmetic  14.1 us (5%)
  local copies, waits for them, and re-layouts  9.02 us (3%)
    pallas_call x3, Pallas kernels, planes_call(): pl.pallas_call(functools.partial(planes_kernel, mode, bands), grid=(steps...  80.4 us
    all_to_all x5, waiting for transfers between devices, swap(): return lax.all_to_all(x, 'ga', split_axis=0, concat_axis=0, tiled=True)  24.6 us
    pallas_call x1, Pallas kernels, per_device(): pl.pallas_call(functools.partial(update_kernel, bands), grid=(steps,), in...  24.2 us
    psum x2, blocking collectives, per_device(): lax.psum((jnp.sum(stats1, axis=2), jnp.sum(proj1, axis=2).T), 'ga')  23.6 us
    all_gather x1, blocking collectives, per_device(): occ = lax.all_gather(psi, 'band', axis=0)  20.2 us
    reduce_scatter x1, waiting for transfers between devices, per_device(): lax.psum_scatter(contribution, 'band', scatter_dimension=1, tiled=True)  20 us
    all_to_all x5, starting transfers between devices, swap(): return lax.all_to_all(x, 'ga', split_axis=0, concat_axis=0, tiled=True)  19.6 us
    pallas_call x1, Pallas kernels, per_device(): pl.pallas_call(functools.partial(rhs_kernel, bands), grid=(steps,), in_sp...  15.3 us
  transfers between devices with their start and end apart: 6, of which 5 were waited for; matrix products, arithmetic and copies ran while one was open for 3% of the time, Pallas kernels for 0%

profile of v1, /device:TPU:0, one launch (start us, length us, event | category | flops | bytes accessed | tf_op | source)
XLA Modules:
  0.0 295.8 jit_solution(13192874704632662510)
XLA Ops:
  7.2 2.3 z_inverse.1
  9.4 5.3 %all-to-all-start = ((f32[8,48,256]{2,1,0:T(8,128)}), f32[8,48,256]{2,1,0:T(8,128)S(1)}, u32[]{:S(2)}, u32[]{:S(2)}) async-start(f32[8,48,256]{2,1,0:T(8,128)} %bitcast.62), calls=%async_computation | async-start | bytes 786432 | tf_op jit(solution)/shard_map/all_to_all | solution.py:416
  14.8 0.8 fusion.1.row
  15.7 1.2 fusion.col1
  16.8 1.0 compare_convert_fusion.col2
  17.9 0.2 reshape.119
  18.1 0.9 pad.7.pot
  19.0 0.1 fusion.17
  19.2 3.9 %all-to-all-done.recv = f32[8,48,256]{2,1,0:T(8,128)S(1)} async-done(((f32[8,48,256]{2,1,0:T(8,128)}), f32[8,48,256]{2,1,0:T(8,128)S(1)}, u32[]{:S(2)}, u32[]{:S(2)}) %all-to-all-start) | async-done | bytes 393248 | tf_op jit(solution)/shard_map/all_to_all | solution.py:416
  23.1 0.7 copy-done.3
  23.8 31.4 %planes_dv.1 = (f32[6,192,512]{2,1,0:T(8,128)}, f32[8,48,256]{2,1,0:T(8,128)}) custom-call(f32[8,48,256]{2,1,0:T(8,128)} %copy-done.3, f32[12,96,128]{2,1,0:T(8,128)} %pad.7.pot, f32[64,2048]{1,0:T(8,128)} %fusion.1.row, bf16[2048,64]{1,0:T(8,128)(2,1)} %fusion.col1, bf16[128,2048]{1,0:T(8,128)(2,1)} %compare_convert_fusion.col2, ...), custom_call_target="tpu_custom_call" | custom-call | tf_op jit(solution)/shard_map/planes_dv/pallas_call | solution.py:246
  55.2 3.6 %all-to-all-start.1 = ((f32[8,48,256]{2,1,0:T(8,128)}), f32[8,48,256]{2,1,0:T(8,128)S(1)}, u32[]{:S(2)}, u32[]{:S(2)}) async-start(f32[8,48,256]{2,1,0:T(8,128)} %get-tuple-element.20), calls=%async_computation.1 | async-start | bytes 786432 | tf_op jit(solution)/shard_map/all_to_all | solution.py:416
  58.8 0.7 broadcast_add_fusion.diag
  59.6 20.2 %all-gather = bf16[8,2,96,256]{3,2,1,0:T(8,128)(2,1)} all-gather(bf16[2,2,96,256]{3,2,1,0:T(8,128)(2,1)S(1)} %copy-done.8), channel_id=2, replica_groups=mesh['ga'=8,'band'=4] {'band'}, dimensions={0}, use_global_device_ids=true | all-gather | bytes 983040 | tf_op jit(solution)/shard_map/all_gather | solution.py:434
  79.8 0.7 copy-done.2
  80.6 3.3 %intersects.1 = (f32[384,256]{1,0:T(8,128)}, f32[32,128]{1,0:T(8,128)}) custom-call(f32[384,256]{1,0:T(8,128)} %bitcast.61, bf16[4,2,2,96,256]{4,3,2,1,0:T(8,128)(2,1)} %bitcast.59, bf16[384,384]{1,0:T(8,128)(2,1)} %constant.126.clone.b_hi, bf16[384,384]{1,0:T(8,128)(2,1)} %constant.127.clone.b_lo), custom_call_target="tpu_custom_call" | custom-call | tf_op jit(solution)/shard_map/intersects/pallas_call | solution.py:439
  83.8 0.8 reduce_sum.104
  84.7 11.8 %psum.49 = f32[32]{0:T(128)S(1)} all-reduce(f32[32]{0:T(128)S(1)} %reduce_sum.104), channel_id=1, replica_groups=mesh['ga'=8,'band'=4] {'ga'}, use_global_device_ids=true, to_apply=%region_1.2 | all-reduce | flops 32 | bytes 256 | tf_op jit(solution)/shard_map/psum | solution.py:446
  96.5 0.5 multiply_bitcast_fusion.parts
  97.0 15.3 %rhs.1 = (f32[2,2,96,256]{3,2,1,0:T(8,128)}, f32[3,2,128]{2,1,0:T(2,128)}, f32[128,4,128]{2,1,0:T(4,128)}, f32[384,256]{1,0:T(8,128)}) custom-call(f32[1,32]{1,0:T(1,128)} %multiply_bitcast_fusion.parts, bf16[4,2,2,96,256]{4,3,2,1,0:T(8,128)(2,1)} %bitcast.60, f32[2,2,96,256]{3,2,1,0:T(8,128)} %bitcast.67, f32[2,96,256]{2,1,0:T(8,128)} %broadcast_add_fusion.diag, ...), custom_call_target="tpu_custom_call" | custom-call | tf_op jit(solution)/shard_map/rhs/pallas_call | solution.py:463
  112.3 3.6 %all-to-all-start.2 = ((f32[8,48,256]{2,1,0:T(8,128)}), f32[8,48,256]{2,1,0:T(8,128)S(1)}, u32[]{:S(2)}, u32[]{:S(2)}) async-start(f32[8,48,256]{2,1,0:T(8,128)} %bitcast.66), calls=%async_computation.2 | async-start | bytes 786432 | tf_op jit(solution)/shard_map/all_to_all | solution.py:416
  115.9 0.2 fusion.11
  116.1 0.1 copy.50
  116.3 0.2 reshape.123
  116.5 0.9 pad.8.pot
  117.3 0.2 reduce_sum.105
  117.6 0.1 reduce_sum.106
  117.7 6.4 %all-to-all-done.2.recv = f32[8,48,256]{2,1,0:T(8,128)S(1)} async-done(((f32[8,48,256]{2,1,0:T(8,128)}), f32[8,48,256]{2,1,0:T(8,128)S(1)}, u32[]{:S(2)}, u32[]{:S(2)}) %all-to-all-start.2) | async-done | bytes 393248 | tf_op jit(solution)/shard_map/all_to_all | solution.py:416
  124.1 0.8 copy-done.5
  124.9 31.6 %planes_local.1 = (f32[6,192,512]{2,1,0:T(8,128)}, f32[6,2,128]{2,1,0:T(2,128)}, f32[12,2,96,128]{3,2,1,0:T(8,128)}, f32[8,48,256]{2,1,0:T(8,128)}) custom-call(f32[8,48,256]{2,1,0:T(8,128)} %copy-done.5, f32[12,96,128]{2,1,0:T(8,128)} %pad.8.pot, f32[64,2048]{1,0:T(8,128)} %fusion.1.row, bf16[2048,64]{1,0:T(8,128)(2,1)} %fusion.col1, ...), custom_call_target="tpu_custom_call" | custom-call | tf_op jit(solution)/shard_map/planes_local/pallas_call | solution.py:246
  156.5 0.8 reduce_sum.107
  157.4 12.1 %all-reduce.3 = (f32[4,128]{1,0:T(4,128)S(1)}, f32[2]{0:T(128)S(1)}, f32[3,2]{1,0:T(4,128)S(1)}) all-reduce(f32[4,128]{1,0:T(4,128)S(1)} %bitcast.70, f32[2]{0:T(128)S(1)} %reduce_sum.107, f32[3,2]{1,0:T(4,128)S(1)} %reduce_sum.106), channel_id=1, replica_groups=mesh['ga'=8,'band'=4] {'ga'}, use_global_device_ids=true, to_apply=%region_3.4 | all-reduce | flops 520 | bytes 4160 | tf_op jit(solution)/shard_map/psum | solution.py:476
  169.5 0.1 reshape.121
  169.6 3.6 %all-to-all-start.3 = ((f32[8,48,256]{2,1,0:T(8,128)}), f32[8,48,256]{2,1,0:T(8,128)S(1)}, u32[]{:S(2)}, u32[]{:S(2)}) async-start(f32[8,48,256]{2,1,0:T(8,128)} %get-tuple-element.28), calls=%async_computation.3 | async-start | bytes 786432 | tf_op jit(solution)/shard_map/all_to_all | solution.py:416
  173.2 0.4 convolution_bitcast_fusion.1
  173.6 0.1 reshape.122.coupled
  173.7 0.1 multiply_reduce_fusion.1
  173.8 0.1 reduce_sum.109
  174.0 0.6 fusion.28.alpha
  174.5 6.8 %all-to-all-done.3 = f32[8,48,256]{2,1,0:T(8,128)S(1)} async-done(((f32[8,48,256]{2,1,0:T(8,128)}), f32[8,48,256]{2,1,0:T(8,128)S(1)}, u32[]{:S(2)}, u32[]{:S(2)}) %all-to-all-start.3) | async-done | bytes 393248 | tf_op jit(solution)/shard_map/all_to_all | solution.py:416
  181.3 0.8 copy-done.4
  182.1 24.2 %update.1 = (f32[2,2,96,256]{3,2,1,0:T(8,128)}, f32[3,2,128]{2,1,0:T(2,128)}, f32[128,4,128]{2,1,0:T(4,128)}, f32[384,256]{1,0:T(8,128)}) custom-call(f32[4,128]{1,0:T(4,128)} %copy-done.13, f32[2]{0:T(128)} %fusion.28.alpha, f32[384,256]{1,0:T(8,128)} %bitcast.63, f32[2,2,96,256]{3,2,1,0:T(8,128)} %get-tuple-element.29.p0, ...), custom_call_target="tpu_custom_call" | custom-call | tf_op jit(solution)/shard_map/update/pallas_call | solution.py:486
  206.3 0.8 reduce_sum.111
  207.0 11.8 %psum.53 = f32[3,2]{1,0:T(4,128)S(1)} all-reduce(f32[3,2]{1,0:T(4,128)S(1)} %reduce_sum.111), channel_id=1, replica_groups=mesh['ga'=8,'band'=4] {'ga'}, use_global_device_ids=true, to_apply=%region_11.12 | all-reduce | flops 6 | bytes 48 | tf_op jit(solution)/shard_map/psum | solution.py:497
  218.8 1.2 reduce_sum.113
  220.0 3.5 %all-to-all-start.4 = ((f32[8,48,256]{2,1,0:T(8,128)}), f32[8,48,256]{2,1,0:T(8,128)S(1)}, u32[]{:S(2)}, u32[]{:S(2)}) async-start(f32[8,48,256]{2,1,0:T(8,128)} %bitcast.65), calls=%async_computation.4 | async-start | bytes 786432 | tf_op jit(solution)/shard_map/all_to_all | solution.py:416
  223.7 0.6 bitcast_divide_fusion.1.rest_2_
  224.3 7.5 %all-to-all-done.4.recv = f32[8,48,256]{2,1,0:T(8,128)S(1)} async-done(((f32[8,48,256]{2,1,0:T(8,128)}), f32[8,48,256]{2,1,0:T(8,128)S(1)}, u32[]{:S(2)}, u32[]{:S(2)}) %all-to-all-start.4) | async-done | bytes 393248 | tf_op jit(solution)/shard_map/all_to_all | solution.py:416
  231.8 0.7 copy-done.1
  232.5 17.4 %planes_next.1 = (f32[6,2,128]{2,1,0:T(2,128)}, f32[12,2,96,128]{3,2,1,0:T(8,128)}) custom-call(f32[8,48,256]{2,1,0:T(8,128)} %copy-done.1, f32[12,96,128]{2,1,0:T(8,128)} %pad.8.pot, f32[64,2048]{1,0:T(8,128)} %fusion.1.row, bf16[2048,64]{1,0:T(8,128)(2,1)} %fusion.col1, bf16[128,2048]{1,0:T(8,128)(2,1)} %compare_convert_fusion.col2, ...), custom_call_target="tpu_custom_call" | custom-call | tf_op jit(solution)/shard_map/planes_next/pallas_call | solution.py:246
  249.9 0.8 reduce_sum.112
  250.7 11.8 %all-reduce.2 = (f32[4,128]{1,0:T(4,128)S(1)}, f32[2]{0:T(128)S(1)}) all-reduce(f32[4,128]{1,0:T(4,128)S(1)} %bitcast.69, f32[2]{0:T(128)S(1)} %reduce_sum.112), channel_id=1, replica_groups=mesh['ga'=8,'band'=4] {'ga'}, use_global_device_ids=true, to_apply=%region_15.16 | all-reduce | flops 514 | bytes 4112 | tf_op jit(solution)/shard_map/psum | solution.py:497
  262.6 0.1 reshape.124
  262.7 0.4 convolution_bitcast_fusion
  263.1 0.1 reshape.125
  263.2 0.1 multiply_reduce_fusion
  263.3 0.1 reduce_sum.115
  263.4 1.7 add_reduce_fusion
  265.2 0.9 broadcast_multiply_fusion
  266.1 0.2 copy-done.6
  266.2 0.3 copy-done.11
  266.5 0.9 multiply_add_fusion
  267.3 20.0 %reduce-scatter.2.cloned.1.call-done = f32[12,24,128]{2,1,0:T(8,128)} async-done(((f32[12,96,128]{2,1,0:T(8,128)}), f32[12,24,128]{2,1,0:T(8,128)}) %reduce-scatter.2.cloned.1.call-update) | async-done | bytes 147472 | tf_op jit(solution)/shard_map/reduce_scatter | solution.py:510
  287.3 1.7 reshape.126
  (51 shorter events, 0.6 us)
Async XLA Ops:
  7.2 108.7 %copy-start = (f32[2,4,4]{2,1,0:T(4,128)S(1)}, f32[2,4,4]{2,1,0:T(4,128)}, u32[]{:S(2)}) copy-start(f32[2,4,4]{2,1,0:T(4,128)} %param.24) | copy-start | bytes 388
  7.2 7.6 %copy-start.14 = (s32[2048]{0:T(1024)S(1)}, s32[2048]{0:T(1024)}, u32[]{:S(2)}) copy-start(s32[2048]{0:T(1024)} %param.26) | copy-start | bytes 24580
  9.4 8.4 %copy-start.9 = (f32[12,9216]{1,0:T(8,128)S(1)}, f32[12,9216]{1,0:T(8,128)}, u32[]{:S(2)}) copy-start(f32[12,9216]{1,0:T(8,128)} %param.22) | copy-start | bytes 1327108
  9.4 13.6 %all-to-all-start = ((f32[8,48,256]{2,1,0:T(8,128)}), f32[8,48,256]{2,1,0:T(8,128)S(1)}, u32[]{:S(2)}, u32[]{:S(2)}) async-start(f32[8,48,256]{2,1,0:T(8,128)} %bitcast.62), calls=%async_computation | async-start | bytes 786432 | tf_op jit(solution)/shard_map/all_to_all | solution.py:416
  19.1 39.7 %copy-start.18 = (f32[2]{0:T(128)S(1)}, f32[2]{0:T(128)}, u32[]{:S(2)}) copy-start(f32[2]{0:T(128)} %param.27) | copy-start | bytes 28
  23.1 0.7 copy-start.3
  55.2 4.4 %copy-start.8 = (bf16[2,2,96,256]{3,2,1,0:T(8,128)(2,1)S(1)}, bf16[2,2,96,256]{3,2,1,0:T(8,128)(2,1)}, u32[]{:S(2)}) copy-start(bf16[2,2,96,256]{3,2,1,0:T(8,128)(2,1)} %param.20) | copy-start | bytes 589828
  55.2 24.6 %all-to-all-start.1 = ((f32[8,48,256]{2,1,0:T(8,128)}), f32[8,48,256]{2,1,0:T(8,128)S(1)}, u32[]{:S(2)}, u32[]{:S(2)}) async-start(f32[8,48,256]{2,1,0:T(8,128)} %get-tuple-element.20), calls=%async_computation.1 | async-start | bytes 786432 | tf_op jit(solution)/shard_map/all_to_all | solution.py:416
  79.8 0.7 copy-start.2
  97.0 18.9 %copy-start.19 = (s32[32]{0:T(128)S(1)}, s32[32]{0:T(128)}, u32[]{:S(2)}) copy-start(s32[32]{0:T(128)} %param.25) | copy-start | bytes 388
  112.3 4.0 %copy-start.10 = (f32[12,9216]{1,0:T(8,128)S(1)}, f32[12,9216]{1,0:T(8,128)}, u32[]{:S(2)}) copy-start(f32[12,9216]{1,0:T(8,128)} %param.21) | copy-start | bytes 1327108
  112.3 11.8 %all-to-all-start.2 = ((f32[8,48,256]{2,1,0:T(8,128)}), f32[8,48,256]{2,1,0:T(8,128)S(1)}, u32[]{:S(2)}, u32[]{:S(2)}) async-start(f32[8,48,256]{2,1,0:T(8,128)} %bitcast.66), calls=%async_computation.2 | async-start | bytes 786432 | tf_op jit(solution)/shard_map/all_to_all | solution.py:416
  116.2 1.1 copy-start.12
  116.2 1.4 copy-start.16
  124.1 0.8 copy-start.5
  169.6 11.7 %all-to-all-start.3 = ((f32[8,48,256]{2,1,0:T(8,128)}), f32[8,48,256]{2,1,0:T(8,128)S(1)}, u32[]{:S(2)}, u32[]{:S(2)}) async-start(f32[8,48,256]{2,1,0:T(8,128)} %get-tuple-element.28), calls=%async_computation.3 | async-start | bytes 786432 | tf_op jit(solution)/shard_map/all_to_all | solution.py:416
  173.7 7.6 %copy-start.13 = (f32[4,128]{1,0:T(4,128)}, f32[4,128]{1,0:T(4,128)S(1)}, u32[]{:S(2)}) copy-start(f32[4,128]{1,0:T(4,128)S(1)} %reshape.122.coupled) | copy-start | bytes 6148
  181.3 0.8 copy-start.4
  220.0 11.7 %all-to-all-start.4 = ((f32[8,48,256]{2,1,0:T(8,128)}), f32[8,48,256]{2,1,0:T(8,128)S(1)}, u32[]{:S(2)}, u32[]{:S(2)}) async-start(f32[8,48,256]{2,1,0:T(8,128)} %bitcast.65), calls=%async_computation.4 | async-start | bytes 786432 | tf_op jit(solution)/shard_map/all_to_all | solution.py:416
  223.5 63.8 %reduce-scatter.2.cloned.1.call-start = ((), (), s32[]{:S(2)}) async-start(), calls=%async_computation.6 | async-start | bytes 737280 | tf_op jit(solution)/shard_map/reduce_scatter | solution.py:510
  231.8 0.7 copy-start.1
  232.5 30.9 %copy-start.15 = (f32[2]{0:T(128)S(1)}, f32[2]{0:T(128)}, u32[]{:S(2)}) copy-start(f32[2]{0:T(128)} %fusion.28.alpha) | copy-start | bytes 28
  232.5 30.9 %copy-start.17 = (f32[2]{0:T(128)S(1)}, f32[2]{0:T(128)}, u32[]{:S(2)}) copy-start(f32[2]{0:T(128)} %bitcast_divide_fusion.1.rest_2_) | copy-start | bytes 28
  232.5 30.9 %copy-start.7 = (f32[12,2,96,128]{3,2,1,0:T(8,128)S(1)}, f32[12,2,96,128]{3,2,1,0:T(8,128)}, u32[]{:S(2)}) copy-start(f32[12,2,96,128]{3,2,1,0:T(8,128)} %get-tuple-element.36) | copy-start | bytes 3538948
  265.1 1.1 copy-start.6
  265.2 1.3 copy-start.11
Sparse Core Ops, SparseCore 0:
  266.2 21.1 reduce-scatter.1

commit v2 on v1

--- a/solution.py
+++ b/solution.py
@@ -214,10 +214,11 @@
 
 
 def planes_call(mode, recv, pot, maps, tables, groups, bands, extra=()):
-    rows, sticks = recv.shape
-    recv = recv.reshape(groups, rows // groups, sticks)
-    local = recv.shape[1]
-    planes = local // (2 * bands)
+    sticks = recv.shape[-1]
+    planes = pot.shape[0]
+    local = planes * 2 * bands
+    rows = groups * local
+    recv = recv.reshape(groups, -1, sticks)
     step = max(1, 8 // (2 * bands))
     if planes % step:
         step = planes
@@ -231,7 +232,7 @@
     quad_shape = jax.ShapeDtypeStruct((steps, bands, LANES), f32)
     dens_spec = pl.BlockSpec((step, bands, GRID, LANES), lambda i: (i, 0, 0, 0))
     dens_shape = jax.ShapeDtypeStruct((planes, bands, GRID, LANES), f32)
-    back_shape = jax.ShapeDtypeStruct(recv.shape, f32)
+    back_shape = jax.ShapeDtypeStruct((groups, local, sticks), f32)
     in_specs = [sticks_spec, pl.BlockSpec((step, GRID, LANES), lambda i: (i, 0, 0))]
     in_specs += [whole(a) for a in maps] + [whole(a) for a in tables]
     if mode == "dv":
@@ -415,6 +416,28 @@
     def swap(x):
         return lax.all_to_all(x, "ga", split_axis=0, concat_axis=0, tiled=True)
 
+    def pack(values, width):
+        line = jnp.concatenate([v.reshape(-1) for v in values])
+        tile = 8 * width
+        line = jnp.pad(line, (0, -line.shape[0] % tile)).reshape(1, -1, width)
+        return jnp.broadcast_to(line, (groups,) + line.shape[1:])
+
+    def unpack(rows, values):
+        line = jnp.sum(rows, axis=0).reshape(-1)
+        out, at = [], 0
+        for v in values:
+            out.append(line[at : at + v.size].reshape(v.shape))
+            at += v.size
+        return out
+
+    def group_sum(*values):
+        return unpack(swap(pack(values, LANES)), values)
+
+    def swap_with(x, *values):
+        x = x.reshape(groups, -1, sticks)
+        both = swap(jnp.concatenate([x, pack(values, sticks)], axis=1))
+        return both, unpack(both[:, x.shape[1] :], values)
+
     start = lax.axis_index("ga") * sticks
     own_xy = lax.dynamic_slice_in_dim(stick_xy, start, sticks)
     freq_z = frequency(jnp.arange(GRID, dtype=jnp.int32))
@@ -431,7 +454,9 @@
         parts = projected.reshape(2 * bands, selected.shape[0], selected.shape[1])
         return jnp.einsum("aij,caj->cai", selected, parts, precision=highest).reshape(2 * bands, nproj)
 
-    occ = lax.all_gather(psi, "band", axis=0)
+    nb = lax.axis_size("band")
+    shifts = [[(i, (i + k) % nb) for i in range(nb)] for k in range(1, nb)]
+    occ = jnp.stack([psi] + [lax.ppermute(psi, "band", ring) for ring in shifts])
     dv_grid, vloc_grid = grid_of(dv), grid_of(vloc)
     along = swap(z_inverse(psi.reshape(flat), t_inv))
     psi_field, back = planes_call("dv", along, dv_grid, maps, tables, groups, bands)
@@ -443,7 +468,7 @@
         name="intersects",
     )(swap(back), occ, *t_fwd)
     inv_norm = 1.0 / (2.0 * GRID * all_sticks)
-    intersect = (lax.psum(jnp.sum(parts, axis=1), "ga") * inv_norm)[None]
+    intersect = (group_sum(jnp.sum(parts, axis=1))[0] * inv_norm)[None]
 
     zt = 16
     steps = GRID // zt
@@ -473,9 +498,10 @@
     p0_field, quad0, dens0, back = planes_call(
         "local", swap(along), vloc_grid, maps, tables, groups, bands, (psi_field,)
     )
-    stats0, proj0, quad0 = lax.psum(
-        (jnp.sum(stats0, axis=2), jnp.sum(proj0, axis=2).T, jnp.sum(quad0, axis=(0, 2))), "ga"
-    )
+    both, (stats0, proj0, quad0) = swap_with(
+        back, jnp.sum(stats0, axis=2), jnp.sum(proj0, axis=2).T, jnp.sum(quad0, axis=(0, 2))
+    )
+    back = both[:, : planes * 2 * bands].reshape(flat)
     coupled0 = couple(proj0)
 
     def band_dot(a, b):
@@ -493,13 +519,13 @@
         scratch_shapes=[pltpu.VMEM(flat, f32), pltpu.VMEM(flat, f32), acc_scratch],
         compiler_params=params(1),
         name="update",
-    )(coupled0, alpha0, swap(back), p0, diag, beta, *t_fwd, *t_inv)
-    stats1, proj1 = lax.psum((jnp.sum(stats1, axis=2), jnp.sum(proj1, axis=2).T), "ga")
+    )(coupled0, alpha0, back, p0, diag, beta, *t_fwd, *t_inv)
+    both, (stats1, proj1) = swap_with(along, jnp.sum(stats1, axis=2), jnp.sum(proj1, axis=2).T)
     ratio = stats1[0] / rr0
     quad1, dens1 = planes_call(
-        "next", swap(along), vloc_grid, maps, tables, groups, bands, (p0_field, psi_field, ratio)
-    )
-    quad1 = lax.psum(jnp.sum(quad1, axis=(0, 2)), "ga")
+        "next", both, vloc_grid, maps, tables, groups, bands, (p0_field, psi_field, ratio)
+    )
+    quad1 = group_sum(jnp.sum(quad1, axis=(0, 2)))[0]
     spread_ratio = jnp.tile(ratio, 2)[:, None]
     proj_p1 = proj1 + spread_ratio * proj0
     diag1 = stats1[1] + ratio * (2.0 * stats1[2] + ratio * stats0[1])
@@ -507,7 +533,8 @@
     wide = lambda a: a[None, :, None, None]
     response = wide(alpha1) * r1 + wide(alpha0 + alpha1 * ratio) * p0
     contribution = 4.0 * jnp.sum(wide(alpha0) * dens0 + wide(alpha1) * dens1, axis=1)
-    density = lax.psum_scatter(contribution, "band", scatter_dimension=1, tiled=True)
+    blocks = contribution.reshape(planes, nb, GRID // nb, LANES).transpose(1, 0, 2, 3)
+    density = jnp.sum(lax.all_to_all(blocks, "band", split_axis=0, concat_axis=0, tiled=True), axis=0)
     return response, density[:, :, :GRID].reshape(planes, -1)
 
 

time: 297 us -> 251 us (0.85)
  blocking collectives: 67.7 us -> 0 us
  starting transfers between devices: 19.7 us -> 34.9 us
  waiting for transfers between devices: 44.6 us -> 58.7 us
  between operations: 14.4 us -> 1.05 us
  other arithmetic: 14.1 us -> 18.3 us
    psum x4 -> x0, blocking collectives: 47.5 us -> none  [the longest x2 23.6 us: per_device(): lax.psum((jnp.sum(stats1, axis=2), jnp.sum(proj1, axis=2).T), 'ga')]
    all_gather x1 -> x0, blocking collectives: 20.2 us -> none  [per_device(): occ = lax.all_gather(psi, 'band', axis=0)]
    reduce_scatter x1 -> x0, waiting for transfers between devices: 20 us -> none  [per_device(): lax.psum_scatter(contribution, 'band', scatter_dimension=1, tiled=True)]
    all_to_all x5 -> x7, waiting for transfers between devices: 24.6 us -> 43.8 us  [swap(): return lax.all_to_all(x, 'ga', split_axis=0, concat_axis=0, tiled=True)]
    all_to_all x0 -> x1, waiting for transfers between devices: none -> 14.9 us  [per_device(): lax.all_to_all(blocks, 'band', split_axis=0, concat_axis=0, tiled=True)]
    ppermute x0 -> x3, starting transfers between devices: none -> 6.14 us  [per_device(): lax.ppermute(psi, 'band', ring)]
    all_to_all x5 -> x7, starting transfers between devices: 19.6 us -> 24.7 us  [swap(): return lax.all_to_all(x, 'ga', split_axis=0, concat_axis=0, tiled=True)]
    all_to_all x0 -> x1, starting transfers between devices: none -> 4.08 us  [per_device(): lax.all_to_all(blocks, 'band', split_axis=0, concat_axis=0, tiled=True)]
  transfers between devices with their start and end apart: 6 -> 11, of which waited for: 5 -> 8; matrix products, arithmetic and copies ran while one was open for 3% -> 4% of each run, Pallas kernels for 0% -> 13%
where the time goes in v2:
time: 251 us; the launch traced here: 250 us
  Pallas kernels  125 us (50%)
  waiting for transfers between devices  58.7 us (23%)
  starting transfers between devices  34.9 us (14%)
  other arithmetic  18.3 us (7%)
  local copies, waits for them, and re-layouts  10.3 us (4%)
    pallas_call x3, Pallas kernels, planes_call(): pl.pallas_call(functools.partial(planes_kernel, mode, bands), grid=(steps...  80.4 us
    all_to_all x7, waiting for transfers between devices, swap(): return lax.all_to_all(x, 'ga', split_axis=0, concat_axis=0, tiled=True)  43.8 us
    all_to_all x7, starting transfers between devices, swap(): return lax.all_to_all(x, 'ga', split_axis=0, concat_axis=0, tiled=True)  24.7 us
    pallas_call x1, Pallas kernels, per_device(): pl.pallas_call(functools.partial(update_kernel, bands), grid=(steps,), in...  24.2 us
    pallas_call x1, Pallas kernels, per_device(): pl.pallas_call(functools.partial(rhs_kernel, bands), grid=(steps,), in_sp...  15.3 us
    all_to_all x1, waiting for transfers between devices, per_device(): lax.all_to_all(blocks, 'band', split_axis=0, concat_axis=0, tiled=True)  14.9 us
    ppermute x3, starting transfers between devices, per_device(): lax.ppermute(psi, 'band', ring)  6.14 us
  transfers between devices with their start and end apart: 11, of which 8 were waited for; matrix products, arithmetic and copies ran while one was open for 4% of the time, Pallas kernels for 13%

profile of v2, /device:TPU:0, one launch (start us, length us, event | category | flops | bytes accessed | tf_op | source)
XLA Modules:
  0.0 249.6 jit_solution(4008298643274596027)
XLA Ops:
  0.7 5.1 %collective-permute-start.2 = (bf16[2,2,96,256]{3,2,1,0:T(8,128)(2,1)}, bf16[2,2,96,256]{3,2,1,0:T(8,128)(2,1)S(1)}, u32[]{:S(2)}, u32[]{:S(2)}) collective-permute-start(bf16[2,2,96,256]{3,2,1,0:T(8,128)(2,1)} %param.20), channel_id=1, source_target_pairs={{0,3},{1,0},{2,1},{3,2},{4,7},{5,4},{6,5},{7,6},{8,11},{9,8},{10,9... | collective-permute-start | bytes 589832 | tf_op jit(solution)/shard_map/ppermute | solution.py:459
  5.8 1.0 collective-permute-start
  6.8 2.2 z_inverse.1
  9.0 3.9 %all-to-all-start = ((f32[8,48,256]{2,1,0:T(8,128)}), f32[8,48,256]{2,1,0:T(8,128)S(1)}, u32[]{:S(2)}, u32[]{:S(2)}) async-start(f32[8,48,256]{2,1,0:T(8,128)} %bitcast.46), calls=%async_computation | async-start | bytes 786432 | tf_op jit(solution)/shard_map/all_to_all | solution.py:417
  12.9 0.2 reshape.184
  13.2 1.1 fusion.col1
  14.3 1.0 compare_convert_fusion.col2
  15.4 0.9 pad.23.pot
  16.3 0.9 fusion.1.row
  17.2 4.0 %all-to-all-done.recv = f32[8,48,256]{2,1,0:T(8,128)S(1)} async-done(((f32[8,48,256]{2,1,0:T(8,128)}), f32[8,48,256]{2,1,0:T(8,128)S(1)}, u32[]{:S(2)}, u32[]{:S(2)}) %all-to-all-start) | async-done | bytes 393248 | tf_op jit(solution)/shard_map/all_to_all | solution.py:417
  21.2 0.7 copy-done.3
  22.0 31.4 %planes_dv.1 = (f32[6,192,512]{2,1,0:T(8,128)}, f32[8,48,256]{2,1,0:T(8,128)}) custom-call(f32[8,48,256]{2,1,0:T(8,128)} %copy-done.3, f32[12,96,128]{2,1,0:T(8,128)} %pad.23.pot, f32[64,2048]{1,0:T(8,128)} %fusion.1.row, bf16[2048,64]{1,0:T(8,128)(2,1)} %fusion.col1, bf16[128,2048]{1,0:T(8,128)(2,1)} %compare_convert_fusion.col2, ...), custom_call_target="tpu_custom_call" | custom-call | tf_op jit(solution)/shard_map/planes_dv/pallas_call | solution.py:247
  53.3 3.5 %all-to-all-start.1 = ((f32[8,48,256]{2,1,0:T(8,128)}), f32[8,48,256]{2,1,0:T(8,128)S(1)}, u32[]{:S(2)}, u32[]{:S(2)}) async-start(f32[8,48,256]{2,1,0:T(8,128)} %get-tuple-element.20), calls=%async_computation.1 | async-start | bytes 786432 | tf_op jit(solution)/shard_map/all_to_all | solution.py:417
  56.9 1.0 pad_maximum_fusion.occ
  57.9 7.1 %all-to-all-done.1 = f32[8,48,256]{2,1,0:T(8,128)S(1)} async-done(((f32[8,48,256]{2,1,0:T(8,128)}), f32[8,48,256]{2,1,0:T(8,128)S(1)}, u32[]{:S(2)}, u32[]{:S(2)}) %all-to-all-start.1) | async-done | bytes 393248 | tf_op jit(solution)/shard_map/all_to_all | solution.py:417
  65.1 0.7 copy-done.2
  65.8 3.3 %intersects.1 = (f32[384,256]{1,0:T(8,128)}, f32[32,128]{1,0:T(8,128)}) custom-call(f32[384,256]{1,0:T(8,128)} %bitcast.45, bf16[4,2,2,96,256]{4,3,2,1,0:T(8,128)(2,1)} %pad_maximum_fusion.occ, bf16[384,384]{1,0:T(8,128)(2,1)} %constant.126.clone.b_hi, bf16[384,384]{1,0:T(8,128)(2,1)} %constant.127.clone.b_lo), custom_call_target="tpu_custom_call" | custom-call | tf_op jit(solution)/shard_map/intersects/pallas_call | solution.py:464
  69.1 0.8 reduce_sum.142
  69.9 0.6 broadcast_in_dim.19
  70.5 3.3 %all-to-all-start.2 = ((f32[8,8,128]{2,1,0:T(8,128)}), f32[8,8,128]{2,1,0:T(8,128)S(1)}, u32[]{:S(2)}, u32[]{:S(2)}) async-start(f32[8,8,128]{2,1,0:T(8,128)} %broadcast_in_dim.19), calls=%async_computation.2 | async-start | bytes 65536 | tf_op jit(solution)/shard_map/all_to_all | solution.py:417
  73.9 0.8 broadcast_add_fusion.diag
  74.6 4.0 %all-to-all-done.2 = f32[8,8,128]{2,1,0:T(8,128)S(1)} async-done(((f32[8,8,128]{2,1,0:T(8,128)}), f32[8,8,128]{2,1,0:T(8,128)S(1)}, u32[]{:S(2)}, u32[]{:S(2)}) %all-to-all-start.2) | async-done | bytes 32800 | tf_op jit(solution)/shard_map/all_to_all | solution.py:417
  78.7 0.5 multiply_bitcast_fusion.parts
  79.2 15.3 %rhs.1 = (f32[2,2,96,256]{3,2,1,0:T(8,128)}, f32[3,2,128]{2,1,0:T(2,128)}, f32[128,4,128]{2,1,0:T(4,128)}, f32[384,256]{1,0:T(8,128)}) custom-call(f32[1,32]{1,0:T(1,128)} %multiply_bitcast_fusion.parts, bf16[4,2,2,96,256]{4,3,2,1,0:T(8,128)(2,1)} %pad_maximum_fusion.occ, f32[2,2,96,256]{3,2,1,0:T(8,128)} %bitcast.53, f32[2,96,256]{2,1,0:T(8,128)} %broadcast_add_fusion.diag, ...), custom_call_target="tpu_custom_call" | custom-call | tf_op jit(solution)/shard_map/rhs/pallas_call | solution.py:488
  94.5 3.6 %all-to-all-start.3 = ((f32[8,48,256]{2,1,0:T(8,128)}), f32[8,48,256]{2,1,0:T(8,128)S(1)}, u32[]{:S(2)}, u32[]{:S(2)}) async-start(f32[8,48,256]{2,1,0:T(8,128)} %bitcast.52), calls=%async_computation.3 | async-start | bytes 786432 | tf_op jit(solution)/shard_map/all_to_all | solution.py:417
  98.1 0.2 reshape.187
  98.3 0.9 pad.25.pot
  99.2 0.2 reduce_sum.145
  99.7 6.7 %all-to-all-done.3.recv = f32[8,48,256]{2,1,0:T(8,128)S(1)} async-done(((f32[8,48,256]{2,1,0:T(8,128)}), f32[8,48,256]{2,1,0:T(8,128)S(1)}, u32[]{:S(2)}, u32[]{:S(2)}) %all-to-all-start.3) | async-done | bytes 393248 | tf_op jit(solution)/shard_map/all_to_all | solution.py:417
  106.3 0.8 copy-done.4
  107.1 31.6 %planes_local.1 = (f32[6,192,512]{2,1,0:T(8,128)}, f32[6,2,128]{2,1,0:T(2,128)}, f32[12,2,96,128]{3,2,1,0:T(8,128)}, f32[8,48,256]{2,1,0:T(8,128)}) custom-call(f32[8,48,256]{2,1,0:T(8,128)} %copy-done.4, f32[12,96,128]{2,1,0:T(8,128)} %pad.25.pot, f32[64,2048]{1,0:T(8,128)} %fusion.1.row, bf16[2048,64]{1,0:T(8,128)(2,1)} %fusion.col1, ...), custom_call_target="tpu_custom_call" | custom-call | tf_op jit(solution)/shard_map/planes_local/pallas_call | solution.py:247
  138.7 0.8 reduce_sum.146
  139.6 1.8 pad_maximum_fusion.1
  141.4 3.7 %all-to-all-start.4 = ((f32[8,56,256]{2,1,0:T(8,128)}), f32[8,56,256]{2,1,0:T(8,128)S(1)}, u32[]{:S(2)}, u32[]{:S(2)}) async-start(f32[8,56,256]{2,1,0:T(8,128)} %pad_maximum_fusion.1), calls=%async_computation.4 | async-start | bytes 917504 | tf_op jit(solution)/shard_map/all_to_all | solution.py:417
  145.1 0.2 fusion.11
  145.3 0.1 copy.74
  145.4 8.6 %all-to-all-done.4 = f32[8,56,256]{2,1,0:T(8,128)S(1)} async-done(((f32[8,56,256]{2,1,0:T(8,128)}), f32[8,56,256]{2,1,0:T(8,128)S(1)}, u32[]{:S(2)}, u32[]{:S(2)}) %all-to-all-start.4) | async-done | bytes 458784 | tf_op jit(solution)/shard_map/all_to_all | solution.py:417
  154.2 0.1 reshape_reshape.3
  154.3 0.4 convolution_bitcast_fusion
  154.6 0.7 reshape.191.coupled
  155.5 0.1 multiply_reduce_fusion
  155.6 0.6 fusion.29.alpha
  156.1 0.8 slice.75
  156.9 24.2 %update.1 = (f32[2,2,96,256]{3,2,1,0:T(8,128)}, f32[3,2,128]{2,1,0:T(2,128)}, f32[128,4,128]{2,1,0:T(4,128)}, f32[384,256]{1,0:T(8,128)}) custom-call(f32[4,128]{1,0:T(4,128)} %reshape.191.coupled, f32[2]{0:T(128)} %fusion.29.alpha, f32[384,256]{1,0:T(8,128)} %bitcast.47, f32[2,2,96,256]{3,2,1,0:T(8,128)} %get-tuple-element.29.p0, ...), custom_call_target="tpu_custom_call" | custom-call | tf_op jit(solution)/shard_map/update/pallas_call | solution.py:512
  181.1 1.2 reduce_sum.150
  182.4 0.8 reduce_sum.149
  183.3 1.8 pad_maximum_fusion.2
  185.1 3.5 %all-to-all-start.5 = ((f32[8,56,256]{2,1,0:T(8,128)}), f32[8,56,256]{2,1,0:T(8,128)S(1)}, u32[]{:S(2)}, u32[]{:S(2)}) async-start(f32[8,56,256]{2,1,0:T(8,128)} %pad_maximum_fusion.2), calls=%async_computation.5 | async-start | bytes 917504 | tf_op jit(solution)/shard_map/all_to_all | solution.py:417
  188.7 8.9 %all-to-all-done.5.recv = f32[8,56,256]{2,1,0:T(8,128)S(1)} async-done(((f32[8,56,256]{2,1,0:T(8,128)}), f32[8,56,256]{2,1,0:T(8,128)S(1)}, u32[]{:S(2)}, u32[]{:S(2)}) %all-to-all-start.5) | async-done | bytes 458784 | tf_op jit(solution)/shard_map/all_to_all | solution.py:417
  198.1 0.1 copy.80
  198.2 0.3 fusion.33
  198.7 17.4 %planes_next.1 = (f32[6,2,128]{2,1,0:T(2,128)}, f32[12,2,96,128]{3,2,1,0:T(8,128)}) custom-call(f32[8,56,256]{2,1,0:T(8,128)} %copy-done.1, f32[12,96,128]{2,1,0:T(8,128)} %pad.25.pot, f32[64,2048]{1,0:T(8,128)} %fusion.1.row, bf16[2048,64]{1,0:T(8,128)(2,1)} %fusion.col1, bf16[128,2048]{1,0:T(8,128)(2,1)} %compare_convert_fusion.col2, ...), custom_call_target="tpu_custom_call" | custom-call | tf_op jit(solution)/shard_map/planes_next/pallas_call | solution.py:247
  216.0 0.8 reduce_sum.152
  216.9 0.6 broadcast_in_dim.26
  217.5 3.3 %all-to-all-start.6 = ((f32[8,8,128]{2,1,0:T(8,128)}), f32[8,8,128]{2,1,0:T(8,128)S(1)}, u32[]{:S(2)}, u32[]{:S(2)}) async-start(f32[8,8,128]{2,1,0:T(8,128)} %broadcast_in_dim.26), calls=%async_computation.6 | async-start | bytes 65536 | tf_op jit(solution)/shard_map/all_to_all | solution.py:417
  220.8 0.1 fusion.9
  221.1 4.5 %all-to-all-done.6 = f32[8,8,128]{2,1,0:T(8,128)S(1)} async-done(((f32[8,8,128]{2,1,0:T(8,128)}), f32[8,8,128]{2,1,0:T(8,128)S(1)}, u32[]{:S(2)}, u32[]{:S(2)}) %all-to-all-start.6) | async-done | bytes 32800 | tf_op jit(solution)/shard_map/all_to_all | solution.py:417
  225.6 0.7 multiply_add_fusion.2
  226.3 1.7 add_reduce_fusion
  228.1 0.8 copy.83
  228.9 4.1 %all-to-all-start.7 = ((f32[4,12,24,128]{3,2,1,0:T(8,128)}), f32[4,12,24,128]{3,2,1,0:T(8,128)S(1)}, u32[]{:S(2)}, u32[]{:S(2)}) async-start(f32[4,12,24,128]{3,2,1,0:T(8,128)} %copy.83), calls=%async_computation.7 | async-start | bytes 1179648 | tf_op jit(solution)/shard_map/all_to_all | solution.py:537
  233.0 0.9 multiply_add_fusion
  233.9 14.9 %all-to-all-done.7 = f32[4,12,24,128]{3,2,1,0:T(8,128)S(1)} async-done(((f32[4,12,24,128]{3,2,1,0:T(8,128)}), f32[4,12,24,128]{3,2,1,0:T(8,128)S(1)}, u32[]{:S(2)}, u32[]{:S(2)}) %all-to-all-start.7) | async-done | bytes 589856 | tf_op jit(solution)/shard_map/all_to_all | solution.py:537
  248.8 0.8 reshape.201
  (77 shorter events, 1.9 us)
Async XLA Ops:
  0.6 144.5 %copy-start = (f32[2,4,4]{2,1,0:T(4,128)S(1)}, f32[2,4,4]{2,1,0:T(4,128)}, u32[]{:S(2)}) copy-start(f32[2,4,4]{2,1,0:T(4,128)} %param.24) | copy-start | bytes 388
  0.6 12.3 %copy-start.8 = (f32[12,9216]{1,0:T(8,128)S(1)}, f32[12,9216]{1,0:T(8,128)}, u32[]{:S(2)}) copy-start(f32[12,9216]{1,0:T(8,128)} %param.22) | copy-start | bytes 1327108
  0.7 56.2 %collective-permute-start.2 = (bf16[2,2,96,256]{3,2,1,0:T(8,128)(2,1)}, bf16[2,2,96,256]{3,2,1,0:T(8,128)(2,1)S(1)}, u32[]{:S(2)}, u32[]{:S(2)}) collective-permute-start(bf16[2,2,96,256]{3,2,1,0:T(8,128)(2,1)} %param.20), channel_id=1, source_target_pairs={{0,3},{1,0},{2,1},{3,2},{4,7},{5,4},{6,5},{7,6},{8,11},{9,8},{10,9... | collective-permute-start | bytes 589832 | tf_op jit(solution)/shard_map/ppermute | solution.py:459
  5.8 51.1 %collective-permute-start.1 = (bf16[2,2,96,256]{3,2,1,0:T(8,128)(2,1)}, bf16[2,2,96,256]{3,2,1,0:T(8,128)(2,1)S(1)}, u32[]{:S(2)}, u32[]{:S(2)}) collective-permute-start(bf16[2,2,96,256]{3,2,1,0:T(8,128)(2,1)} %param.20), channel_id=1, source_target_pairs={{0,2},{1,3},{2,0},{3,1},{4,6},{5,7},{6,4},{7,5},{8,10},{9,11},{10,... | collective-permute-start | bytes 589832 | tf_op jit(solution)/shard_map/ppermute | solution.py:459
  5.8 51.1 %collective-permute-start = (bf16[2,2,96,256]{3,2,1,0:T(8,128)(2,1)}, bf16[2,2,96,256]{3,2,1,0:T(8,128)(2,1)S(1)}, u32[]{:S(2)}, u32[]{:S(2)}) collective-permute-start(bf16[2,2,96,256]{3,2,1,0:T(8,128)(2,1)} %param.20), channel_id=1, source_target_pairs={{0,1},{1,2},{2,3},{3,0},{4,5},{5,6},{6,7},{7,4},{8,9},{9,10},{10,1... | collective-permute-start | bytes 589832 | tf_op jit(solution)/shard_map/ppermute | solution.py:459
  9.0 4.1 %copy-start.12 = (s32[2048]{0:T(1024)S(1)}, s32[2048]{0:T(1024)}, u32[]{:S(2)}) copy-start(s32[2048]{0:T(1024)} %param.26) | copy-start | bytes 24580
  9.0 12.2 %all-to-all-start = ((f32[8,48,256]{2,1,0:T(8,128)}), f32[8,48,256]{2,1,0:T(8,128)S(1)}, u32[]{:S(2)}, u32[]{:S(2)}) async-start(f32[8,48,256]{2,1,0:T(8,128)} %bitcast.46), calls=%async_computation | async-start | bytes 786432 | tf_op jit(solution)/shard_map/all_to_all | solution.py:417
  17.2 39.7 %copy-start.7 = (bf16[2,2,96,256]{3,2,1,0:T(8,128)(2,1)S(1)}, bf16[2,2,96,256]{3,2,1,0:T(8,128)(2,1)}, u32[]{:S(2)}) copy-start(bf16[2,2,96,256]{3,2,1,0:T(8,128)(2,1)} %param.20) | copy-start | bytes 589828
  21.2 0.7 copy-start.3
  53.3 11.7 %all-to-all-start.1 = ((f32[8,48,256]{2,1,0:T(8,128)}), f32[8,48,256]{2,1,0:T(8,128)S(1)}, u32[]{:S(2)}, u32[]{:S(2)}) async-start(f32[8,48,256]{2,1,0:T(8,128)} %get-tuple-element.20), calls=%async_computation.1 | async-start | bytes 786432 | tf_op jit(solution)/shard_map/all_to_all | solution.py:417
  57.9 15.9 %copy-start.16 = (f32[2]{0:T(128)S(1)}, f32[2]{0:T(128)}, u32[]{:S(2)}) copy-start(f32[2]{0:T(128)} %param.27) | copy-start | bytes 28
  65.1 0.7 copy-start.2
  70.5 8.1 %all-to-all-start.2 = ((f32[8,8,128]{2,1,0:T(8,128)}), f32[8,8,128]{2,1,0:T(8,128)S(1)}, u32[]{:S(2)}, u32[]{:S(2)}) async-start(f32[8,8,128]{2,1,0:T(8,128)} %broadcast_in_dim.19), calls=%async_computation.2 | async-start | bytes 65536 | tf_op jit(solution)/shard_map/all_to_all | solution.py:417
  94.5 3.6 %copy-start.9 = (f32[12,9216]{1,0:T(8,128)S(1)}, f32[12,9216]{1,0:T(8,128)}, u32[]{:S(2)}) copy-start(f32[12,9216]{1,0:T(8,128)} %param.21) | copy-start | bytes 1327108
  94.5 11.8 %all-to-all-start.3 = ((f32[8,48,256]{2,1,0:T(8,128)}), f32[8,48,256]{2,1,0:T(8,128)S(1)}, u32[]{:S(2)}, u32[]{:S(2)}) async-start(f32[8,48,256]{2,1,0:T(8,128)} %bitcast.52), calls=%async_computation.3 | async-start | bytes 786432 | tf_op jit(solution)/shard_map/all_to_all | solution.py:417
  98.1 1.1 copy-start.11
  98.1 1.4 copy-start.14
  106.3 0.8 copy-start.4
  138.7 6.4 %copy-start.17 = (s32[32]{0:T(128)S(1)}, s32[32]{0:T(128)}, u32[]{:S(2)}) copy-start(s32[32]{0:T(128)} %param.25) | copy-start | bytes 388
  141.4 12.6 %all-to-all-start.4 = ((f32[8,56,256]{2,1,0:T(8,128)}), f32[8,56,256]{2,1,0:T(8,128)S(1)}, u32[]{:S(2)}, u32[]{:S(2)}) async-start(f32[8,56,256]{2,1,0:T(8,128)} %pad_maximum_fusion.1), calls=%async_computation.4 | async-start | bytes 917504 | tf_op jit(solution)/shard_map/all_to_all | solution.py:417
  185.1 12.4 %all-to-all-start.5 = ((f32[8,56,256]{2,1,0:T(8,128)}), f32[8,56,256]{2,1,0:T(8,128)S(1)}, u32[]{:S(2)}, u32[]{:S(2)}) async-start(f32[8,56,256]{2,1,0:T(8,128)} %pad_maximum_fusion.2), calls=%async_computation.5 | async-start | bytes 917504 | tf_op jit(solution)/shard_map/all_to_all | solution.py:417
  197.6 1.1 copy-start.1
  197.6 1.0 copy-start.15
  198.6 27.0 %copy-start.13 = (f32[2]{0:T(128)S(1)}, f32[2]{0:T(128)}, u32[]{:S(2)}) copy-start(f32[2]{0:T(128)} %fusion.29.alpha) | copy-start | bytes 28
  198.7 27.7 %copy-start.6 = (f32[12,2,96,128]{3,2,1,0:T(8,128)S(1)}, f32[12,2,96,128]{3,2,1,0:T(8,128)}, u32[]{:S(2)}) copy-start(f32[12,2,96,128]{3,2,1,0:T(8,128)} %get-tuple-element.36) | copy-start | bytes 3538948
  217.5 8.1 %all-to-all-start.6 = ((f32[8,8,128]{2,1,0:T(8,128)}), f32[8,8,128]{2,1,0:T(8,128)S(1)}, u32[]{:S(2)}, u32[]{:S(2)}) async-start(f32[8,8,128]{2,1,0:T(8,128)} %broadcast_in_dim.26), calls=%async_computation.6 | async-start | bytes 65536 | tf_op jit(solution)/shard_map/all_to_all | solution.py:417
  228.1 5.0 %copy-start.5 = (f32[2,2,96,256]{3,2,1,0:T(8,128)S(1)}, f32[2,2,96,256]{3,2,1,0:T(8,128)}, u32[]{:S(2)}) copy-start(f32[2,2,96,256]{3,2,1,0:T(8,128)} %get-tuple-element.29.p0) | copy-start | bytes 1179652
  228.1 4.9 %copy-start.10 = (f32[2,2,96,256]{3,2,1,0:T(8,128)S(1)}, f32[2,2,96,256]{3,2,1,0:T(8,128)}, u32[]{:S(2)}) copy-start(f32[2,2,96,256]{3,2,1,0:T(8,128)} %get-tuple-element.35) | copy-start | bytes 1179652
  228.9 19.9 %all-to-all-start.7 = ((f32[4,12,24,128]{3,2,1,0:T(8,128)}), f32[4,12,24,128]{3,2,1,0:T(8,128)S(1)}, u32[]{:S(2)}, u32[]{:S(2)}) async-start(f32[4,12,24,128]{3,2,1,0:T(8,128)} %copy.83), calls=%async_computation.7 | async-start | bytes 1179648 | tf_op jit(solution)/shard_map/all_to_all | solution.py:537
